TPU v7x, 16 devices: a 4x2x1 block of a 4x4x8 slice. The times are simulated.
16 devices in a mesh: dp: 2 (over y, z), tp: 8 (over x, core).
Axes of the slice: x: 4, y: 2, z: 1, core: 2. Of those that a mesh axis runs over, the one named last changes fastest.
The devices are a block of a 4x4x8 slice.
Arguments:
- x_in: bfloat16 [8192, 2048], P(('dp', 'tp')), parts along dimension 0
- dy_in: bfloat16 [8192, 2048], P(('dp', 'tp')), parts along dimension 0
- w_q: bfloat16 [2048, 8, 256], P(None, 'tp')
- w_k: bfloat16 [2048, 1, 256], replicated
- w_v: bfloat16 [2048, 1, 256], replicated
- w_o: bfloat16 [8, 256, 2048], P('tp')
Outputs:
- output 1: bfloat16 [8192, 2048], P(('dp', 'tp')), parts along dimension 0
- output 2: float32 [4096, 8, 256], P('dp', 'tp'), parts along dimension 0
- output 3: float32 [16, 256, 2048], P(('dp', 'tp')), parts along dimension 0
- output 4: float32 [4096, 256], P(('dp', 'tp')), parts along dimension 0
- output 5: float32 [4096, 256], P(('dp', 'tp')), parts along dimension 0
There are 2 independent parts. A program takes and returns all parts, laid end to end along the dimension named above; an argument that names none is the same for every part.
All inputs are finite; a program needn't handle non-finite values.
Results may differ from a plain program's by a relative error of at most 0.0101431.
Values are sent between devices in bfloat16 or wider.
A program may use at most 768 MiB of HBM per device.

v0:
```python
import jax
import jax.numpy as jnp
from jax import lax
from jax.sharding import PartitionSpec as P


def solution(mesh):
    n_model = mesh.shape["tp"]

    def local_grads(x_blk, dy_blk, wq_loc, w_k, w_v, wo_loc):
        f32 = jnp.float32
        bf16 = jnp.bfloat16
        model_dim, kv_heads, head_dim = w_k.shape
        repl = n_model // kv_heads
        scale = head_dim ** -0.5
        dev_idx = lax.axis_index("tp")
        kv_index = dev_idx // repl
        wk_loc = lax.dynamic_index_in_dim(w_k, kv_index, axis=1, keepdims=False)
        wv_loc = lax.dynamic_index_in_dim(w_v, kv_index, axis=1, keepdims=False)
        x_full = lax.all_gather(x_blk, "tp", axis=0, tiled=True)
        dy_full = lax.all_gather(dy_blk, "tp", axis=0, tiled=True)
        tokens = x_full.shape[0]
        queries = jnp.einsum("tc,che->hte", x_full, wq_loc, preferred_element_type=f32).astype(bf16)
        key_rows = jnp.dot(x_full, wk_loc, preferred_element_type=f32).astype(bf16)
        val_rows = jnp.dot(x_full, wv_loc, preferred_element_type=f32).astype(bf16)
        causal = lax.broadcasted_iota(jnp.int32, (tokens, tokens), 0) >= lax.broadcasted_iota(jnp.int32, (tokens, tokens), 1)
        scores = jnp.einsum("hqe,ke->hqk", queries, key_rows, preferred_element_type=f32) * scale
        scores = jnp.where(causal, scores, -jnp.inf)
        attn_prob = jax.nn.softmax(scores, axis=-1)
        prob_bf = attn_prob.astype(bf16)
        attn_out = jnp.einsum("hqk,ke->hqe", prob_bf, val_rows, preferred_element_type=f32).astype(bf16)
        d_out = jnp.einsum("tc,hec->hte", dy_full, wo_loc, preferred_element_type=f32).astype(bf16)
        grad_wo = jnp.einsum("hte,tc->hec", attn_out, dy_full, preferred_element_type=f32)
        d_prob = jnp.einsum("hqe,ke->hqk", d_out, val_rows, preferred_element_type=f32)
        delta_row = jnp.einsum("hqe,hqe->hq", d_out, attn_out, preferred_element_type=f32)[..., None]
        d_score = (attn_prob * (d_prob - delta_row)).astype(bf16)
        d_query = (jnp.einsum("hqk,ke->hqe", d_score, key_rows, preferred_element_type=f32) * scale).astype(bf16)
        d_key = (jnp.einsum("hqk,hqe->ke", d_score, queries, preferred_element_type=f32) * scale).astype(bf16)
        d_val = jnp.einsum("hqk,hqe->ke", prob_bf, d_out, preferred_element_type=f32).astype(bf16)
        grad_wq = jnp.einsum("tc,hte->che", x_full, d_query, preferred_element_type=f32)
        dx_part = (jnp.einsum("hte,che->tc", d_query, wq_loc, preferred_element_type=f32)
                   + jnp.einsum("te,ce->tc", d_key, wk_loc, preferred_element_type=f32)
                   + jnp.einsum("te,ce->tc", d_val, wv_loc, preferred_element_type=f32))
        dx_blk = lax.psum_scatter(dx_part, "tp", scatter_dimension=0, tiled=True).astype(bf16)
        slot = (jnp.arange(kv_heads) == kv_index)[:, None, None]
        wk_part = jnp.einsum("tc,te->ce", x_full, d_key, preferred_element_type=f32)
        wv_part = jnp.einsum("tc,te->ce", x_full, d_val, preferred_element_type=f32)
        wk_buf = jnp.where(slot, wk_part[None], 0.0).reshape(kv_heads * model_dim, head_dim)
        wv_buf = jnp.where(slot, wv_part[None], 0.0).reshape(kv_heads * model_dim, head_dim)
        dwk_blk = lax.psum_scatter(wk_buf, "tp", scatter_dimension=0, tiled=True)
        dwv_blk = lax.psum_scatter(wv_buf, "tp", scatter_dimension=0, tiled=True)
        return dx_blk, grad_wq, grad_wo, dwk_blk, dwv_blk

    tok_spec = P(("dp", "tp"))
    return jax.shard_map(
        local_grads,
        mesh=mesh,
        in_specs=(tok_spec, tok_spec, P(None, "tp", None), P(), P(), P("tp")),
        out_specs=(tok_spec, P("dp", "tp", None), tok_spec, tok_spec, tok_spec),
        check_vma=False,
    )
```

profile of v0, /device:TPU:113, one launch (start us, length us, event | category | flops | bytes accessed | tf_op | source)
XLA Modules:
  0.0 657.5 jit_solution(1292902820643803830)
XLA Ops:
  7.3 0.7 all-gather.5.cloned.1.call-update
  8.1 0.7 all-gather.3.cloned.1.call-update
  8.9 85.2 %all-gather.5.cloned.1.call-done = bf16[4096,2048]{1,0:T(8,128)(2,1)} async-done(((bf16[512,2048]{1,0:T(8,128)(2,1)}), bf16[4096,2048]{1,0:T(8,128)(2,1)}) %all-gather.5.cloned.1.call-update) | async-done | bytes 16777232 | tf_op jit(solution)/shard_map/all_gather | solution.py:21
  94.1 10.6 %fusion.10 = bf16[4096,256]{0,1:T(8,128)(2,1)S(1)} fusion(bf16[4096,2048]{1,0:T(8,128)(2,1)} %all-gather.5.cloned.1.call-done, bf16[1,256,2048]{2,1,0:T(8,128)(2,1)} %param.11), kind=kOutput, calls=%fused_computation.18 | convolution fusion | flops 4296015872 | bytes 19922944 | tf_op jit(solution)/shard_map/tc,hec->hte/dot_general | solution.py:32
  104.7 3.1 copy.19
  107.8 69.5 %all-gather.3.cloned.1.call-done = bf16[4096,2048]{1,0:T(8,128)(2,1)} async-done(((bf16[512,2048]{1,0:T(8,128)(2,1)}), bf16[4096,2048]{1,0:T(8,128)(2,1)}) %all-gather.3.cloned.1.call-update) | async-done | bytes 16777232 | tf_op jit(solution)/shard_map/all_gather | solution.py:20
  177.3 9.6 %convolution_convert_fusion = bf16[4096,256]{1,0:T(8,128)(2,1)} fusion(bf16[4096,2048]{1,0:T(8,128)(2,1)} %all-gather.3.cloned.1.call-done, bf16[2048,1,256]{2,0,1:T(8,128)(2,1)S(1)} %copy-done), kind=kOutput, calls=%fused_computation.14 | convolution fusion | flops 4296015872 | bytes 19922944 | tf_op jit(solution)/shard_map/dot_general | solution.py:24
  187.0 12.0 %fusion.9 = bf16[4096,256]{0,1:T(8,128)(2,1)} fusion(bf16[4096,2048]{1,0:T(8,128)(2,1)} %all-gather.3.cloned.1.call-done, bf16[2048,1,256]{2,0,1:T(8,128)(2,1)} %param.8), kind=kOutput, calls=%fused_computation.17 | convolution fusion | flops 4296015872 | bytes 19922944 | tf_op jit(solution)/shard_map/tc,che->hte/dot_general | solution.py:23
  198.9 28.2 %fusion.26 = (f32[4096]{0:T(1024)S(1)}, f32[4096,4096]{1,0:T(8,128)}) fusion(bf16[4096,256]{0,1:T(8,128)(2,1)} %fusion.9, bf16[4096,256]{1,0:T(8,128)(2,1)} %convolution_convert_fusion), kind=kOutput, calls=%fused_computation.38 | convolution fusion | flops 8657039360 | bytes 71319552 | tf_op jit(solution)/shard_map/hqe,ke->hqk/dot_general | solution.py:27
  227.2 21.1 %fusion.1 = f32[4096]{0:T(1024)S(1)} fusion(f32[4096,4096]{1,0:T(8,128)} %get-tuple-element.11, f32[4096]{0:T(1024)S(1)} %get-tuple-element.10), kind=kLoop, calls=%fused_computation.5 | loop fusion | flops 33550336 | bytes 67141632 | tf_op jit(solution)/shard_map/reduce_sum | solution.py:29
  248.3 25.3 %fusion.6 = bf16[4096,256]{1,0:T(8,128)(2,1)S(1)} fusion(bf16[4096,256]{0,1:T(8,128)(2,1)} %copy-done.3, f32[4096,4096]{1,0:T(8,128)} %get-tuple-element.11, f32[4096]{0:T(1024)S(1)} %fusion.1, f32[4096]{0:T(1024)S(1)} %get-tuple-element.10), kind=kOutput, calls=%fused_computation.13 | convolution fusion | flops 8641314816 | bytes 71335936 | tf_op jit(solution)/shard_map/hqk,hqe->ke/dot_general | solution.py:39
  273.6 1.4 copy-done.1
  274.9 10.1 %fusion.11 = f32[2048,256]{0,1:T(8,128)} fusion(bf16[4096,256]{1,0:T(8,128)(2,1)S(1)} %fusion.6, bf16[4096,2048]{1,0:T(8,128)(2,1)} %all-gather.3.cloned.1.call-done, pred[]{:T(512)S(6)} %eq.5), kind=kOutput, calls=%fused_computation.23 | convolution fusion | flops 4295491584 | bytes 20971520 | tf_op jit(solution)/shard_map/tc,te->ce/dot_general | solution.py:47
  285.2 10.1 %fusion.15 = f32[4096,256]{1,0:T(8,128)} fusion(bf16[4096,2048]{1,0:T(8,128)(2,1)} %all-gather.3.cloned.1.call-done, bf16[2048,1,256]{2,0,1:T(8,128)(2,1)S(1)} %copy-done.5), kind=kOutput, calls=%fused_computation.28 | convolution fusion | flops 4294967296 | bytes 22020096 | tf_op jit(solution)/shard_map/dot_general | solution.py:25
  295.3 35.3 %online-softmax = f32[4096,256]{1,0:T(8,128)} custom-call(f32[4096,4096]{1,0:T(8,128)} %get-tuple-element.11, f32[4096,256]{1,0:T(8,128)} %fusion.15), custom_call_target="tpu_custom_call" | custom-call | tf_op online-softmax
  330.5 4.2 multiply_reduce_fusion
  334.7 0.4 copy-done.2
  335.2 0.7 copy-done.4
  335.8 41.0 %multiply_convert_fusion = bf16[4096,4096]{1,0:T(8,128)(2,1)} fusion(f32[4096]{0:T(1024)S(1)} %multiply_reduce_fusion, bf16[4096,256]{0,1:T(8,128)(2,1)S(1)} %copy-done.4, f32[4096,256]{1,0:T(8,128)S(1)} %copy-done.2, f32[4096]{0:T(1024)S(1)} %fusion.1, f32[4096,4096]{1,0:T(8,128)} %get-tuple-element.11, f32[4096]{0:T(1024)S(1)} %get-tuple-element.10), kind=kOutput, calls=%fused_computation | convolution fusion | flops 8674869248 | bytes 107003904 | tf_op jit(solution)/shard_map/hqe,ke->hqk/dot_general | solution.py:34
  376.8 16.1 %fusion.5 = bf16[4096,256]{1,0:T(8,128)(2,1)S(1)} fusion(bf16[4096,4096]{1,0:T(8,128)(2,1)} %multiply_convert_fusion, bf16[4096,256]{0,1:T(8,128)(2,1)S(1)} %copy-done.6), kind=kOutput, calls=%fused_computation.12 | convolution fusion | flops 8592031744 | bytes 37748736 | tf_op jit(solution)/shard_map/hqk,hqe->ke/dot_general | solution.py:38
  393.0 9.7 %fusion.12 = f32[2048,256]{0,1:T(8,128)} fusion(bf16[4096,256]{1,0:T(8,128)(2,1)S(1)} %fusion.5, bf16[4096,2048]{1,0:T(8,128)(2,1)} %all-gather.3.cloned.1.call-done, pred[]{:T(512)S(6)} %eq.5), kind=kOutput, calls=%fused_computation.25 | convolution fusion | flops 4295491584 | bytes 20971520 | tf_op jit(solution)/shard_map/tc,te->ce/dot_general | solution.py:46
  402.7 13.2 %fusion.18 = f32[4096,2048]{1,0:T(8,128)} fusion(bf16[4096,256]{1,0:T(8,128)(2,1)S(1)} %fusion.5, bf16[2048,1,256]{2,0,1:T(8,128)(2,1)S(1)} %copy-done), kind=kOutput, calls=%fused_computation.31 | convolution fusion | flops 4294967296 | bytes 36700160 | tf_op jit(solution)/shard_map/te,ce->tc/dot_general | solution.py:42
  415.9 15.5 %fusion.4 = bf16[4096,256]{1,0:T(8,128)(2,1)S(1)} fusion(bf16[4096,4096]{1,0:T(8,128)(2,1)} %multiply_convert_fusion, bf16[4096,256]{1,0:T(8,128)(2,1)S(1)} %copy-done.7), kind=kOutput, calls=%fused_computation.11 | convolution fusion | flops 8592031744 | bytes 37748736 | tf_op jit(solution)/shard_map/hqk,ke->hqe/dot_general | solution.py:37
  431.5 14.4 %fusion.21 = f32[4096,2048]{1,0:T(8,128)} fusion(bf16[4096,256]{1,0:T(8,128)(2,1)S(1)} %fusion.4, bf16[2048,1,256]{2,0,1:T(8,128)(2,1)} %param.8), kind=kOutput, calls=%fused_computation.34 | convolution fusion | flops 4294967296 | bytes 36700160 | tf_op jit(solution)/shard_map/hte,che->tc/dot_general | solution.py:41
  445.9 34.6 %add_add_fusion = f32[4096,2048]{1,0:T(8,128)} fusion(f32[4096,2048]{1,0:T(8,128)} %fusion.21, f32[4096,2048]{1,0:T(8,128)} %fusion.18, bf16[4096,256]{1,0:T(8,128)(2,1)} %copy-done.1, bf16[2048,1,256]{2,0,1:T(8,128)(2,1)} %param.10), kind=kOutput, calls=%fused_computation.6 | convolution fusion | flops 4311744512 | bytes 103809024 | tf_op jit(solution)/shard_map/te,ce->tc/dot_general | solution.py:43
  480.5 9.5 %convolution_bitcast_fusion.1 = f32[2048,1,256]{0,2,1:T(8,128)} fusion(bf16[4096,256]{1,0:T(8,128)(2,1)S(1)} %fusion.4, bf16[4096,2048]{1,0:T(8,128)(2,1)} %all-gather.3.cloned.1.call-done), kind=kOutput, calls=%fused_computation.21 | convolution fusion | flops 4294967296 | bytes 20971520 | tf_op jit(solution)/shard_map/tc,hte->che/dot_general | solution.py:40
  490.0 6.0 copy.12
  496.0 12.9 %convolution_bitcast_fusion = f32[1,256,2048]{2,1,0:T(8,128)} fusion(bf16[4096,2048]{1,0:T(8,128)(2,1)} %all-gather.5.cloned.1.call-done, f32[4096,256]{1,0:T(8,128)} %online-softmax), kind=kOutput, calls=%fused_computation.20 | convolution fusion | flops 4296015872 | bytes 23068672 | tf_op jit(solution)/shard_map/hte,tc->hec/dot_general | solution.py:33
  508.9 1.8 copy.14
  510.7 1.8 copy.13
  512.5 134.3 %reduce-scatter.4.cloned.1.call-done = f32[512,2048]{1,0:T(8,128)} async-done(((f32[4096,2048]{1,0:T(8,128)}), f32[512,2048]{1,0:T(8,128)}) %reduce-scatter.4.cloned.1.call-update) | async-done | bytes 4194320 | tf_op jit(solution)/shard_map/reduce_scatter | solution.py:44
  646.8 3.8 convert_element_type.63
  (23 shorter events, 0.5 us)
Async XLA Ops:
  7.2 170.1 %copy-start = (bf16[2048,1,256]{2,0,1:T(8,128)(2,1)S(1)}, bf16[2048,1,256]{2,0,1:T(8,128)(2,1)}, u32[]{:S(2)}) copy-start(bf16[2048,1,256]{2,0,1:T(8,128)(2,1)} %param.9) | copy-start | bytes 3145732
  7.2 86.9 %all-gather.5.cloned.1.call-start = ((), (), s32[]{:S(2)}) async-start(), calls=%async_computation.4 | async-start | bytes 18874368 | tf_op jit(solution)/shard_map/all_gather | solution.py:21
  8.0 169.3 %all-gather.3.cloned.1.call-start = ((), (), s32[]{:S(2)}) async-start(), calls=%async_computation.3 | async-start | bytes 18874368 | tf_op jit(solution)/shard_map/all_gather | solution.py:20
  8.8 500.1 %reduce-scatter.8.cloned.1.call-start = ((), (), s32[]{:S(2)}) async-start(), calls=%async_computation.7 | async-start | bytes 2359296 | tf_op jit(solution)/shard_map/reduce_scatter | solution.py:51
  104.7 82.3 %copy-start.3 = (bf16[4096,256]{0,1:T(8,128)(2,1)}, bf16[4096,256]{0,1:T(8,128)(2,1)S(1)}, u32[]{:S(2)}) copy-start(bf16[4096,256]{0,1:T(8,128)(2,1)S(1)} %fusion.10) | copy-start | bytes 6291460
  273.6 1.4 copy-start.1
  274.9 10.2 %copy-start.5 = (bf16[2048,1,256]{2,0,1:T(8,128)(2,1)S(1)}, bf16[2048,1,256]{2,0,1:T(8,128)(2,1)}, u32[]{:S(2)}) copy-start(bf16[2048,1,256]{2,0,1:T(8,128)(2,1)} %param.10) | copy-start | bytes 3145732
  285.1 225.6 %reduce-scatter.6.cloned.1.call-start = ((), (), s32[]{:S(2)}) async-start(), calls=%async_computation.6 | async-start | bytes 2359296 | tf_op jit(solution)/shard_map/reduce_scatter | solution.py:50
  330.5 4.6 copy-start.2
  330.5 5.3 copy-start.4
  335.8 41.0 %copy-start.6 = (bf16[4096,256]{0,1:T(8,128)(2,1)S(1)}, bf16[4096,256]{0,1:T(8,128)(2,1)}, u32[]{:S(2)}) copy-start(bf16[4096,256]{0,1:T(8,128)(2,1)} %fusion.9) | copy-start | bytes 6291460
  402.7 13.2 %copy-start.7 = (bf16[4096,256]{1,0:T(8,128)(2,1)S(1)}, bf16[4096,256]{1,0:T(8,128)(2,1)}, u32[]{:S(2)}) copy-start(bf16[4096,256]{1,0:T(8,128)(2,1)} %convolution_convert_fusion) | copy-start | bytes 6291460
  431.4 215.3 %reduce-scatter.4.cloned.1.call-start = ((), (), s32[]{:S(2)}) async-start(), calls=%async_computation.5 | async-start | bytes 37748736 | tf_op jit(solution)/shard_map/reduce_scatter | solution.py:44
Sparse Core Ops, SparseCore 0:
  9.6 84.3 all-gather.4
  95.7 81.6 all-gather.2
  285.2 26.8 reduce-scatter.7
  431.6 26.8 reduce-scatter.5
  480.6 166.0 reduce-scatter.3
where the time goes:
time: 667 us; the launch traced here: 658 us
  waiting for transfers between devices  291 us (44%)
  matrix products  273 us (41%)
  Pallas kernels  35.3 us (5%)
  other arithmetic  29.1 us (4%)
  local copies, waits for them, and re-layouts  15.2 us (2%)
  between operations  14.3 us (2%)
    reduce_scatter x1, waiting for transfers between devices, local_grads(): lax.psum_scatter(dx_part, 'tp', scatter_dimension=0, tiled=True)  134 us
    all_gather x1, waiting for transfers between devices, local_grads(): dy_full = lax.all_gather(dy_blk, 'tp', axis=0, tiled=True)  85.2 us
    all_gather x1, waiting for transfers between devices, local_grads(): x_full = lax.all_gather(x_blk, 'tp', axis=0, tiled=True)  69.5 us
    dot_general x1, matrix products, local_grads(): jnp.einsum('hqe,ke->hqk', d_out, val_rows, preferred_element_type=f32)  41 us
    unnamed x1, Pallas kernels  35.3 us
    dot_general x1, matrix products, local_grads(): jnp.einsum('te,ce->tc', d_val, wv_loc, preferred_element_type=f32)  34.6 us
    dot_general x1, matrix products, local_grads(): jnp.einsum('hqe,ke->hqk', queries, key_rows, preferred_element_type=f32)  28.2 us
    dot_general x1, matrix products, local_grads(): jnp.einsum('hqk,hqe->ke', prob_bf, d_out, preferred_element_type=f32)  25.3 us
  transfers between devices with their start and end apart: 5, of which 3 were waited for; matrix products, arithmetic and copies ran while one was open for 31% of the time, Pallas kernels for 5%

commit v1 on v0

v1 whole, which is shorter than its diff:
```python
import functools

import jax
import jax.numpy as jnp
from jax import lax
from jax.experimental import pallas as pl
from jax.experimental.pallas import tpu as pltpu
from jax.sharding import PartitionSpec as P

MESH = pl.DeviceIdType.MESH
F32 = jnp.float32
BF16 = jnp.bfloat16
LOG2E = 1.4426950408889634
VMEM_MAX = 67_043_328


def _mm(a, b):
    return lax.dot_general(a, b, (((1,), (0,)), ((), ())), preferred_element_type=F32)


def _mm_t(a, b):
    return lax.dot_general(a, b, (((1,), (1,)), ((), ())), preferred_element_type=F32)


def _ring(n):
    me = lax.axis_index("tp")
    core = lax.rem(me, 2)
    right = lax.rem(me + 2, n)
    left = lax.rem(me + n - 2, n)
    opp = lax.rem(me + n // 2, n)
    mate = me + 1 - 2 * core
    return me, core, right, left, opp, mate


def _barrier(devices):
    barrier = pltpu.get_barrier_semaphore()
    for d in devices:
        pl.semaphore_signal(barrier, inc=1, device_id={"tp": d}, device_id_type=MESH)
    pl.semaphore_wait(barrier, len(devices))


def _remote(src, dst, ssem, rsem, dev):
    return pltpu.make_async_remote_copy(
        src_ref=src, dst_ref=dst, send_sem=ssem, recv_sem=rsem,
        device_id={"tp": dev}, device_id_type=MESH)


def _gather_kernel(n, x, dy, wq, wk, wv, wo, xf, dyf, q, k, v, do,
                   buf, ssem_r, ssem_l, ssem_p, rsem, lsem, osem):
    me, core, right, left, opp, mate = _ring(n)
    rows = x.shape[0]
    half = rows // 2
    flip = 1 - 2 * core
    srcs, dsts = (x, dy), (xf, dyf)
    _barrier((left, right, mate))

    def view(a, blk, h):
        return dsts[a].at[blk, pl.ds(h * half, half)]

    def send(src, a, blk, h, ssem, dev):
        c = _remote(src, view(a, blk, h), ssem, rsem.at[a, blk * 2 + h], dev)
        c.start()
        sends.append(c)

    def recv(a, blk, h):
        _remote(view(a, blk, h), view(a, blk, h), ssem_p.at[a, 0],
                rsem.at[a, blk * 2 + h], mate).wait_recv()

    sends = []
    for a in range(2):
        for i, h in enumerate((0, 1)):
            own = srcs[a].at[pl.ds(h * half, half)]
            send(own, a, me, h, ssem_r.at[a, i], right)
            own = srcs[a].at[pl.ds((1 - h) * half, half)]
            send(own, a, me, 1 - h, ssem_l.at[a, i], left)
        for h in range(2):
            own = srcs[a].at[pl.ds(h * half, half)]
            send(own, a, me, h, ssem_p.at[a, h], mate)

    def project(a, b0, h0, b1, h1):
        def body(i, _):
            side, par = lax.rem(i, 2), i // 2
            blk = b0 + side * (b1 - b0) + par * flip
            h = h0 + side * (h1 - h0)
            pltpu.make_async_copy(view(a, blk, h), buf.at[i], lsem.at[i]).wait()
            at = pl.ds(pl.multiple_of(blk * rows + h * half, half), half)
            data = buf[i]
            if a == 0:
                q[at] = _mm(data, wq[...]).astype(BF16)
                k[at] = _mm(data, wk[...]).astype(BF16)
                v[at] = _mm(data, wv[...]).astype(BF16)
            else:
                do[at] = _mm_t(data, wo[...]).astype(BF16)
            return _
        lax.fori_loop(0, 4, body, 0)

    def first(a):
        for h in range(2):
            pltpu.make_async_copy(srcs[a].at[pl.ds(h * half, half)], buf.at[h], lsem.at[h]).start()
        for h in range(2):
            recv(a, mate, h)
            pltpu.make_async_copy(view(a, mate, h), buf.at[2 + h], lsem.at[2 + h]).start()
        project(a, me, 0, me, 1)
        outs = [pltpu.make_async_copy(buf.at[h], view(a, me, h), osem.at[h]) for h in range(2)]
        for c in outs:
            c.start()
        for c in outs:
            c.wait()

    def event(a, e):
        b0, h0, b1, h1 = ((left, 0, right, 1), (left, 1, right, 0), (opp, 0, opp, 1))[e - 1]
        recv(a, b0, h0)
        if e == 1:
            send(view(a, b0, h0), a, b0, h0, ssem_r.at[a, 2], right)
        send(view(a, b0, h0), a, b0, h0, ssem_p.at[a, 2 * e], mate)
        pltpu.make_async_copy(view(a, b0, h0), buf.at[0], lsem.at[0]).start()
        recv(a, b1, h1)
        if e == 1:
            send(view(a, b1, h1), a, b1, h1, ssem_l.at[a, 2], left)
        send(view(a, b1, h1), a, b1, h1, ssem_p.at[a, 2 * e + 1], mate)
        pltpu.make_async_copy(view(a, b1, h1), buf.at[1], lsem.at[1]).start()
        for i, (b, h) in enumerate(((b0, h0), (b1, h1))):
            recv(a, b + flip, h)
            pltpu.make_async_copy(view(a, b + flip, h), buf.at[2 + i], lsem.at[2 + i]).start()
        project(a, b0, h0, b1, h1)

    first(0)
    first(1)
    for a, e in ((0, 1), (0, 2), (1, 1), (1, 2), (0, 3), (1, 3)):
        event(a, e)
    for c in sends:
        c.wait_send()


def _grad_kernel(n, scale, q, k, v, do, xf, dyf, wq, wk, wv,
                 dx, dwq, dwo, dwk, dwv, wqf,
                 s_ref, p_ref, acc, lhs, dqs, dqr, kvr, kvx, dwr, dwx, xbuf,
                 mrow, lrow, oacc, qt, dot_,
                 w_sr, w_sl, w_sp, w_recv, dq_send, dq_recv, kv_send, kv_recv,
                 rs_send, rs_recv, x_sem, b_sem):
    me, core, right, left, opp, mate = _ring(n)
    chip = me // 2
    flip = 1 - 2 * core
    blk, width = q.shape[1], q.shape[2]
    model = dwq.shape[0]
    tile = model // (n // 2)
    lanes = 128
    whalf = model // 2
    _barrier([lax.rem(me + d, n) for d in range(1, n)])
    sends = []

    def wview(b, h):
        return wqf.at[b, pl.ds(h * whalf, whalf)]

    def wsend(src, b, h, ssem, dev):
        _remote(src, wview(b, h), ssem, w_recv.at[b * 2 + h], dev).start()

    def wrecv(b, h):
        _remote(wview(b, h), wview(b, h), w_sp.at[0], w_recv.at[b * 2 + h], mate).wait_recv()

    for i, h in enumerate((0, 1)):
        wsend(wq.at[pl.ds(h * whalf, whalf)], me, h, w_sr.at[i], right)
        wsend(wq.at[pl.ds((1 - h) * whalf, whalf)], me, 1 - h, w_sl.at[i], left)
    for h in range(2):
        wsend(wq.at[pl.ds(h * whalf, whalf)], me, h, w_sp.at[h], mate)

    def wevent(e):
        b0, h0, b1, h1 = ((left, 0, right, 1), (left, 1, right, 0), (opp, 0, opp, 1))[e - 1]
        wrecv(b0, h0)
        wrecv(b1, h1)
        if e == 1:
            wsend(wview(b0, h0), b0, h0, w_sr.at[2], right)
            wsend(wview(b1, h1), b1, h1, w_sl.at[2], left)
        wsend(wview(b0, h0), b0, h0, w_sp.at[2 * e], mate)
        wsend(wview(b1, h1), b1, h1, w_sp.at[2 * e + 1], mate)

    acc[...] = jnp.zeros_like(acc)
    dwo[...] = jnp.zeros_like(dwo)

    def fold(val, op):
        out = val[:, :lanes]
        for c in range(1, val.shape[1] // lanes):
            out = op(out, val[:, c * lanes:(c + 1) * lanes])
        return out

    def q_step(t, carry):
        nb = lax.rem(me + 1 + t, n)
        dy_copy = pltpu.make_async_copy(dyf.at[nb], xbuf.at[0], x_sem.at[0])
        dy_copy.start()
        qn = q[nb]
        don = do[nb]
        qt[...] = qn.T
        dot_[...] = don.T
        mrow[...] = jnp.full_like(mrow, -jnp.inf)

        def scores(j, _):
            sc = _mm_t(q[nb], k[j])
            s_ref[j] = sc
            mrow[...] = jnp.maximum(mrow[...], fold(sc, jnp.maximum))
            return _

        lax.fori_loop(0, nb, scores, 0)
        sc = _mm_t(qn, k[nb])
        keep = (lax.broadcasted_iota(jnp.int32, sc.shape, 0)
                >= lax.broadcasted_iota(jnp.int32, sc.shape, 1))
        sc = jnp.where(keep, sc, -jnp.inf)
        s_ref[nb] = sc
        m = jnp.max(jnp.maximum(mrow[...], fold(sc, jnp.maximum)), axis=1, keepdims=True)
        mrow[...] = jnp.broadcast_to(m, mrow.shape)
        lrow[...] = jnp.zeros_like(lrow)

        def expo(j, _):
            pr = jnp.exp2((s_ref[j] - mrow[:, :1]) * (scale * LOG2E))
            s_ref[j] = pr
            lrow[...] += fold(pr, jnp.add)
            return _

        lax.fori_loop(0, nb + 1, expo, 0)
        inv = 1.0 / jnp.sum(lrow[...], axis=1, keepdims=True)
        lrow[...] = jnp.broadcast_to(inv, lrow.shape)
        oacc[...] = jnp.zeros_like(oacc)

        def values(j, _):
            pb = (s_ref[j] * lrow[:, :1]).astype(BF16)
            p_ref[j] = pb
            oacc[...] += _mm(pb, v[j])
            return _

        lax.fori_loop(0, nb + 1, values, 0)
        ob = oacc[...].astype(BF16)
        delta = jnp.sum(don.astype(F32) * ob.astype(F32), axis=1, keepdims=True)
        mrow[...] = jnp.broadcast_to(delta, mrow.shape)
        oacc[...] = jnp.zeros_like(oacc)

        def grads(j, _):
            dp = _mm_t(do[nb], v[j])
            ds = (s_ref[j] * lrow[:, :1] * (dp - mrow[:, :1])).astype(BF16)
            oacc[...] += _mm(ds, k[j])
            acc[0, j] += _mm(qt[...], ds)
            acc[1, j] += _mm(dot_[...], p_ref[j])
            return _

        lax.fori_loop(0, nb + 1, grads, 0)
        dq = (oacc[...] * scale).astype(BF16)
        dqs[nb] = dq
        lhs[nb, 0:width] = dq.T

        @pl.when(t < n - 1)
        def _():
            _remote(dqs.at[nb], dqr.at[me], dq_send.at[nb], dq_recv.at[me], nb).start()

        @pl.when(t == n - 1)
        def _():
            dqr[me] = dq

        @pl.when(t == 3)
        def _():
            wevent(1)

        @pl.when(t == 5)
        def _():
            wevent(2)

        dy_copy.wait()
        ot = ob.T
        for c in range(model // tile):
            at = pl.ds(c * tile, tile)
            dwo[:, at] += _mm(ot, xbuf[0, :, at])
        return carry

    lax.fori_loop(0, n, q_step, 0)

    f_mine = jnp.where(core == 0, scale, 1.0).astype(F32)
    f_other = jnp.where(core == 0, 1.0, scale).astype(F32)

    def kv_copy(b):
        return _remote(p_ref.at[b, pl.ds(0, width)], lhs.at[b, pl.ds(2 * width, width)],
                       kv_send.at[b], kv_recv.at[b], mate)

    def convert(i, _):
        b = lax.rem(me - core + n // 2 + i, n)
        p_ref[b, 0:width] = (acc[1 - core, b] * f_other).astype(BF16)
        kv_copy(b).start()
        lhs[b, width:2 * width] = (acc[core, b] * f_mine).astype(BF16)
        return _

    lax.fori_loop(0, n, convert, 0)

    half_chips = n // 2

    def stag(b):
        return s_ref.at[half_chips + b // 2, pl.ds(lax.rem(b, 2) * width, width)]

    def pair(b):
        kv_copy(b).wait_recv()
        stag(b)[...] = (lhs[b, width:2 * width].astype(F32)
                        + lhs[b, 2 * width:3 * width].astype(F32))

    base = 2 * chip
    ob_, rb, lb = opp - core, right - core, left - core

    def rs_copy(src, dst, r, side, kind):
        return _remote(src, dst.at[side, kind], rs_send.at[r, side, kind],
                       rs_recv.at[r, side, kind], right if side == 0 else left)

    def rs_start(*args):
        c = rs_copy(*args)
        c.start()
        sends.append(c)

    def rs_wait(dst, r, side, kind):
        rs_copy(dst.at[side, kind], dst, r, side, kind).wait_recv()

    pair(ob_)
    rs_start(stag(ob_), kvr, 0, 0, 0)
    pair(ob_ + 1)
    rs_start(stag(ob_ + 1), kvr, 0, 1, 0)
    pair(rb + 1)
    rs_start(stag(rb + 1), kvr, 0, 0, 2)
    pair(lb)
    rs_start(stag(lb), kvr, 0, 1, 2)
    for b in (rb, lb + 1, base, base + 1):
        pair(b)

    def x_copy(b, slot):
        return pltpu.make_async_copy(xf.at[b], xbuf.at[slot], x_sem.at[slot])

    x_copy(0, 0).start()

    def x_step(b, carry):
        slot = lax.rem(b, 2)
        x_copy(b, slot).wait()

        @pl.when(b < n - 1)
        def _():
            x_copy(b + 1, 1 - slot).start()

        for c in range(model // tile):
            xt = xbuf[slot, :, c * tile:(c + 1) * tile]
            acc[0, c] += _mm(lhs[b, 0:width], xt)
            acc[1, c] += _mm(lhs[b, width:2 * width], xt) + _mm(lhs[b, 2 * width:3 * width], xt)
        return carry

    def clear(c, _):
        acc[0, c] = jnp.zeros_like(acc[0, c])
        acc[1, c] = jnp.zeros_like(acc[1, c])
        return _

    lax.fori_loop(0, half_chips, clear, 0)
    lax.fori_loop(0, n, x_step, 0)
    wevent(3)

    rs_wait(kvr, 0, 0, 0)
    stag(rb)[...] += kvr[0, 0]
    rs_start(stag(rb), kvr, 0, 0, 1)
    rs_wait(kvr, 0, 1, 0)
    stag(lb + 1)[...] += kvr[1, 0]
    rs_start(stag(lb + 1), kvr, 0, 1, 1)

    def part(b):
        return acc.at[1, b // 2, :, pl.ds(lax.rem(b, 2) * (tile // 2), tile // 2)]

    def part_cols(h):
        return slice(h * (tile // 2), (h + 1) * (tile // 2))

    rs_start(acc.at[1, ob_ // 2, :, pl.ds(0, tile // 2)], dwr, 1, 0, 0)
    rs_start(acc.at[1, ob_ // 2, :, pl.ds(tile // 2, tile // 2)], dwr, 1, 1, 0)
    rs_start(acc.at[1, rb // 2, :, pl.ds(tile // 2, tile // 2)], dwr, 1, 0, 2)
    rs_start(acc.at[1, lb // 2, :, pl.ds(0, tile // 2)], dwr, 1, 1, 2)

    for b in range(n):
        kv_copy(b).wait_send()
    for e, (b0, h0, b1, h1) in enumerate(((mate, 0, mate, 1), (left + flip, 0, right + flip, 1),
                                          (left + flip, 1, right + flip, 0), (opp + flip, 0, opp + flip, 1))):
        wrecv(b0, h0)
        wrecv(b1, h1)
    for d in range(1, n):
        peer = lax.rem(me + d, n)
        _remote(dqr.at[peer], dqr.at[peer], dq_send.at[peer], dq_recv.at[peer], peer).wait_recv()

    def w_copy(h, c, slot):
        return pltpu.make_async_copy(wqf.at[h, pl.ds(c * tile, tile)],
                                     p_ref.at[h, :, pl.ds(slot * width, width)], b_sem.at[slot, h])

    def own_copy(c, slot):
        return pltpu.make_async_copy(wq.at[pl.ds(c * tile, tile)],
                                     p_ref.at[me, :, pl.ds(slot * width, width)], b_sem.at[slot, me])

    def w_load(c, slot):
        own_copy(c, slot).start()
        for d in range(1, n):
            w_copy(lax.rem(me + d, n), c, slot).start()

    w_load(0, 0)
    for c in range(model // tile):
        slot = c % 2
        for h in range(n):
            w_copy(h, c, slot).wait()
        if c + 1 < model // tile:
            w_load(c + 1, 1 - slot)
        s_ref[c] = jnp.zeros_like(s_ref[c])

        def heads(h, _):
            s_ref[c] += _mm_t(dqr[h], p_ref[h, :, slot * width:(slot + 1) * width])
            return _

        lax.fori_loop(0, n, heads, 0)

    rs_wait(dwr, 1, 0, 0)
    acc[1, rb // 2, :, part_cols(0)] += dwr[0, 0]
    rs_start(acc.at[1, rb // 2, :, pl.ds(0, tile // 2)], dwr, 1, 0, 1)
    rs_wait(dwr, 1, 1, 0)
    acc[1, lb // 2, :, part_cols(1)] += dwr[1, 0]
    rs_start(acc.at[1, lb // 2, :, pl.ds(tile // 2, tile // 2)], dwr, 1, 1, 1)

    for c in range(model // tile):
        dwq[c * tile:(c + 1) * tile] = acc[0, c].T

    rs_wait(kvr, 0, 0, 1)
    rs_wait(kvr, 0, 1, 2)
    stag(base)[...] += kvr[0, 1] + kvr[1, 2]
    rs_wait(kvr, 0, 0, 2)
    rs_wait(kvr, 0, 1, 1)
    stag(base + 1)[...] += kvr[0, 2] + kvr[1, 1]
    swap = _remote(stag(mate), kvx.at[0], b_sem.at[2, 0], b_sem.at[2, 1], mate)
    swap.start()
    kvx[1] = stag(me)[...]
    swap.wait()
    kv_first = kvx[1 - core].T
    kv_second = kvx[core].T

    def split(val):
        hi = val.astype(BF16)
        rest = val - hi.astype(F32)
        mid = rest.astype(BF16)
        lo = (rest - mid.astype(F32)).astype(BF16)
        return hi, mid, lo

    for d in range(1, n):
        peer = lax.rem(me + d, n)
        _remote(dqr.at[peer], dqr.at[peer], dq_send.at[peer], dq_recv.at[peer], peer).wait_send()
    for i, parts in enumerate((split(kv_first), split(kv_second))):
        for g, val in enumerate(parts):
            dqs[3 * i + g] = val
    for c in range(model // tile):
        at = slice(c * tile, (c + 1) * tile)
        total = s_ref[c]
        for i, w in enumerate((wk, wv)):
            wt = w[at]
            total += (_mm_t(dqs[3 * i + 2], wt) + _mm_t(dqs[3 * i + 1], wt)) + _mm_t(dqs[3 * i], wt)
        dx[:, at] = total.astype(BF16)

    rs_wait(dwr, 1, 0, 1)
    rs_wait(dwr, 1, 1, 2)
    acc[1, base // 2, :, part_cols(0)] += dwr[0, 1] + dwr[1, 2]
    rs_wait(dwr, 1, 0, 2)
    rs_wait(dwr, 1, 1, 1)
    acc[1, base // 2, :, part_cols(1)] += dwr[0, 2] + dwr[1, 1]
    swap = _remote(part(mate), dwx.at[0], b_sem.at[2, 2], b_sem.at[2, 3], mate)
    swap.start()
    dwx[1] = part(me)[...]
    swap.wait()
    dwk[...] = dwx[1 - core].T
    dwv[...] = dwx[core].T

    for c in sends:
        c.wait_send()
    for i in range(3):
        _remote(wview(me, 0), wview(me, 0), w_sr.at[i], w_recv.at[0], mate).wait_send()
        _remote(wview(me, 0), wview(me, 0), w_sl.at[i], w_recv.at[0], mate).wait_send()
    for i in range(8):
        _remote(wview(me, 0), wview(me, 0), w_sp.at[i], w_recv.at[0], mate).wait_send()


def solution(mesh):
    n = mesh.shape["tp"]
    vmem = pl.BlockSpec(memory_space=pltpu.VMEM)
    hbm = pl.BlockSpec(memory_space=pl.ANY)
    dma = pltpu.SemaphoreType.DMA

    def local_grads(x_blk, dy_blk, wq_loc, w_k, w_v, wo_loc):
        model, kv_heads, width = w_k.shape
        rows = x_blk.shape[0]
        scale = width ** -0.5
        wq2 = wq_loc.reshape(model, width)
        wk2 = w_k.reshape(model, width)
        wv2 = w_v.reshape(model, width)
        wo2 = wo_loc.reshape(width, model)
        full = jax.ShapeDtypeStruct((n, rows, model), BF16)
        proj = jax.ShapeDtypeStruct((n * rows, width), BF16)
        xf, dyf, q, k, v, do = pl.pallas_call(
            functools.partial(_gather_kernel, n),
            name="gather_project",
            out_shape=(full, full, proj, proj, proj, proj),
            in_specs=[hbm, hbm, vmem, vmem, vmem, vmem],
            out_specs=(hbm, hbm, vmem, vmem, vmem, vmem),
            scratch_shapes=[
                pltpu.VMEM((4, rows // 2, model), BF16),
                dma((2, 3)), dma((2, 3)), dma((2, 8)), dma((2, 2 * n)), dma((4,)), dma((2,)),
            ],
            compiler_params=pltpu.CompilerParams(
                collective_id=0, has_side_effects=True, vmem_limit_bytes=32 * 2 ** 20),
        )(x_blk, dy_blk, wq2, wk2, wv2, wo2)
        q, k, v, do = (a.reshape(n, rows, width) for a in (q, k, v, do))
        tile = 2 * model // n
        dx, dwq, dwo, dwk, dwv, _ = pl.pallas_call(
            functools.partial(_grad_kernel, n, scale),
            name="attention_grads",
            out_shape=(
                jax.ShapeDtypeStruct((rows, model), BF16),
                jax.ShapeDtypeStruct((model, width), F32),
                jax.ShapeDtypeStruct((width, model), F32),
                jax.ShapeDtypeStruct((model // n, width), F32),
                jax.ShapeDtypeStruct((model // n, width), F32),
                jax.ShapeDtypeStruct((n, model, width), BF16),
            ),
            in_specs=[vmem] * 4 + [hbm] * 3 + [vmem] * 2,
            out_specs=(vmem,) * 5 + (hbm,),
            scratch_shapes=[
                pltpu.VMEM((n, rows, rows), F32),
                pltpu.VMEM((n, rows, rows), BF16),
                pltpu.VMEM((2, n, width, rows), F32),
                pltpu.VMEM((n, 3 * width, rows), BF16),
                pltpu.VMEM((n, rows, width), BF16),
                pltpu.VMEM((n, rows, width), BF16),
                pltpu.VMEM((2, 3, width, rows), F32),
                pltpu.VMEM((2, width, rows), F32),
                pltpu.VMEM((2, 3, width, tile // 2), F32),
                pltpu.VMEM((2, width, tile // 2), F32),
                pltpu.VMEM((2, rows, model), BF16),
                pltpu.VMEM((rows, 128), F32),
                pltpu.VMEM((rows, 128), F32),
                pltpu.VMEM((rows, width), F32),
                pltpu.VMEM((width, rows), BF16),
                pltpu.VMEM((width, rows), BF16),
                dma((3,)), dma((3,)), dma((8,)), dma((2 * n,)),
                dma((n,)), dma((n,)), dma((n,)), dma((n,)),
                dma((2, 2, 3)), dma((2, 2, 3)), dma((2,)), dma((3, n)),
            ],
            compiler_params=pltpu.CompilerParams(
                collective_id=1, has_side_effects=True, vmem_limit_bytes=VMEM_MAX),
        )(q, k, v, do, xf, dyf, wq2, wk2, wv2)
        return (dx, dwq.reshape(model, 1, width), dwo.reshape(1, width, model), dwk, dwv)

    tok_spec = P(("dp", "tp"))
    return jax.shard_map(
        local_grads,
        mesh=mesh,
        in_specs=(tok_spec, tok_spec, P(None, "tp", None), P(), P(), P("tp")),
        out_specs=(tok_spec, P("dp", "tp", None), tok_spec, tok_spec, tok_spec),
        check_vma=False,
    )
```

time: 667 us -> 312 us (0.47); the launches traced: 658 us -> 312 us
  waiting for transfers between devices: 291 us -> 0 us
  matrix products: 273 us -> 0 us
  Pallas kernels: 35.3 us -> 287 us
  other arithmetic: 29.1 us -> 0 us
  between operations: 14.3 us -> 0.69 us
  local copies, waits for them, and re-layouts: 15.2 us -> 23.4 us
    pallas_call x0 -> x2, Pallas kernels: none -> 287 us  [the longest x1 147 us: local_grads(): pl.pallas_call(functools.partial(_gather_kernel, n), name='gather_project...]
    dot_general x16 -> x0, matrix products: 273 us -> none  [the longest x1 41 us: local_grads(): jnp.einsum('hqe,ke->hqk', d_out, val_rows, preferred_element_type=f32)]
    all_gather x2 -> x0, waiting for transfers between devices: 155 us -> none  [the longest x1 85.2 us: local_grads(): dy_full = lax.all_gather(dy_blk, 'tp', axis=0, tiled=True)]
    reduce_scatter x3 -> x0, waiting for transfers between devices: 134 us -> none  [the longest x1 134 us: local_grads(): lax.psum_scatter(dx_part, 'tp', scatter_dimension=0, tiled=True)]
    unnamed x1 -> x0, Pallas kernels: 35.3 us -> none
    reduce_sum x1 -> x0, other arithmetic: 21.1 us -> none  [local_grads(): attn_prob = jax.nn.softmax(scores, axis=-1)]
    unnamed x20 -> x33, local copies, waits for them, and re-layouts: 15.2 us -> 23.4 us
  transfers between devices with their start and end apart: 5 -> 0, of which waited for: 3 -> 0; matrix products, arithmetic and copies ran while one was open for 31% -> 0% of each run, Pallas kernels for 5% -> 0%
where the time goes in v1:
time: 312 us
  Pallas kernels  287 us (92%)
  local copies, waits for them, and re-layouts  23.4 us (8%)
    pallas_call x1, Pallas kernels, local_grads(): pl.pallas_call(functools.partial(_gather_kernel, n), name='gather_project...  147 us
    pallas_call x1, Pallas kernels, local_grads(): pl.pallas_call(functools.partial(_grad_kernel, n, scale), name='attention...  141 us
    unnamed x33, local copies, waits for them, and re-layouts  23.4 us

profile of v1, /device:TPU:113, one launch (start us, length us, event | category | flops | bytes accessed | tf_op | source)
XLA Modules:
  0.0 311.6 jit_solution(5141141772300890792)
XLA Ops:
  0.6 0.0 copy-start
  0.6 1.2 copy-done
  1.9 0.0 copy-start.1
  1.9 1.2 copy-done.1
  3.1 0.0 copy-start.2
  3.1 1.2 copy-done.2
  4.3 0.0 copy-start.7
  4.3 1.6 copy-done.7
  5.9 0.0 copy-start.8
  5.9 1.6 copy-done.8
  7.5 0.0 copy-start.9
  7.5 1.2 copy-done.9
  8.7 146.9 %gather_project.1 = (bf16[8,512,2048]{2,1,0:T(8,128)(2,1)}, bf16[8,512,2048]{2,1,0:T(8,128)(2,1)}, bf16[4096,256]{1,0:T(8,128)(2,1)S(1)}, bf16[4096,256]{1,0:T(8...) custom-call(bf16[512,2048]{1,0:T(8,128)(2,1)S(1)} %copy-done.7, ...), custom_call_target="tpu_custom_call" | custom-call | tf_op jit(solution)/shard_map/gather_project/pallas_call | solution.py:491
  155.7 0.0 copy-start.3
  155.7 1.3 copy-done.3
  157.0 0.0 copy-start.4
  157.0 1.3 copy-done.4
  158.3 0.0 copy-start.5
  158.3 1.3 copy-done.5
  159.6 0.0 copy-start.6
  159.6 1.4 copy-done.6
  161.0 140.5 %attention_grads.1 = (bf16[512,2048]{1,0:T(8,128)(2,1)}, f32[2048,256]{1,0:T(8,128)}, f32[256,2048]{1,0:T(8,128)}, f32[256,256]{1,0:T(8,128)}, f32[256,256]{1,0:T(8,128)}, /*index=5*/bf16[8,2048,256]{2,1,0:T(8,128)(2,1)}) custom-call(bf16[8,512,256]{2,1,0:T(8,128)(2,1)} %bitcast.16, bf16[8,512,256]{2,1,0:T(8,128)(2,1)} %bitcast.17, ...), custom_call_target="tpu_custom_call" | custom-call | tf_op jit(solution)/shard_map/attention_grads/pallas_call | solution.py:506
  301.6 0.0 copy-start.11
  301.6 4.9 %copy.11 = f32[2048,1,256]{2,1,0:T(1,128)} copy(f32[2048,1,256]{2,0,1:T(8,128)} %bitcast.22) | data formatting | bytes 4194304
  306.5 0.0 copy-done.11
  306.5 1.3 copy.16
  307.8 1.0 copy-done.10
  308.9 1.3 copy.17
  310.2 0.0 copy-done.13
  310.2 0.7 copy.18
  310.9 0.0 copy-done.12
  310.9 0.7 copy.19
  (3 shorter events, 0.0 us)
Async XLA Ops:
  0.6 1.2 copy-start
  1.9 1.2 copy-start.1
  3.1 1.2 copy-start.2
  4.3 1.6 copy-start.7
  5.9 1.6 copy-start.8
  7.5 1.2 copy-start.9
  155.7 1.3 copy-start.3
  157.0 1.3 copy-start.4
  158.3 1.3 copy-start.5
  159.6 1.4 copy-start.6
  301.6 4.9 %copy-start.11 = (bf16[512,2048]{1,0:T(8,128)(2,1)S(1)}, bf16[512,2048]{1,0:T(8,128)(2,1)}, u32[]{:S(2)}) copy-start(bf16[512,2048]{1,0:T(8,128)(2,1)} %get-tuple-element.37) | copy-start | bytes 6291460
  306.5 2.3 copy-start.10
  308.9 1.3 copy-start.13
  308.9 2.0 copy-start.12

commit v2 on v1

--- a/solution.py
+++ b/solution.py
@@ -45,110 +45,94 @@
         device_id={"tp": dev}, device_id_type=MESH)
 
 
-def _gather_kernel(n, x, dy, wq, wk, wv, wo, xf, dyf, q, k, v, do,
-                   buf, ssem_r, ssem_l, ssem_p, rsem, lsem, osem):
-    me, core, right, left, opp, mate = _ring(n)
-    rows = x.shape[0]
-    half = rows // 2
-    flip = 1 - 2 * core
-    srcs, dsts = (x, dy), (xf, dyf)
-    _barrier((left, right, mate))
-
-    def view(a, blk, h):
-        return dsts[a].at[blk, pl.ds(h * half, half)]
-
-    def send(src, a, blk, h, ssem, dev):
-        c = _remote(src, view(a, blk, h), ssem, rsem.at[a, blk * 2 + h], dev)
-        c.start()
-        sends.append(c)
-
-    def recv(a, blk, h):
-        _remote(view(a, blk, h), view(a, blk, h), ssem_p.at[a, 0],
-                rsem.at[a, blk * 2 + h], mate).wait_recv()
-
-    sends = []
-    for a in range(2):
-        for i, h in enumerate((0, 1)):
-            own = srcs[a].at[pl.ds(h * half, half)]
-            send(own, a, me, h, ssem_r.at[a, i], right)
-            own = srcs[a].at[pl.ds((1 - h) * half, half)]
-            send(own, a, me, 1 - h, ssem_l.at[a, i], left)
-        for h in range(2):
-            own = srcs[a].at[pl.ds(h * half, half)]
-            send(own, a, me, h, ssem_p.at[a, h], mate)
-
-    def project(a, b0, h0, b1, h1):
-        def body(i, _):
-            side, par = lax.rem(i, 2), i // 2
-            blk = b0 + side * (b1 - b0) + par * flip
-            h = h0 + side * (h1 - h0)
-            pltpu.make_async_copy(view(a, blk, h), buf.at[i], lsem.at[i]).wait()
-            at = pl.ds(pl.multiple_of(blk * rows + h * half, half), half)
-            data = buf[i]
-            if a == 0:
-                q[at] = _mm(data, wq[...]).astype(BF16)
-                k[at] = _mm(data, wk[...]).astype(BF16)
-                v[at] = _mm(data, wv[...]).astype(BF16)
-            else:
-                do[at] = _mm_t(data, wo[...]).astype(BF16)
-            return _
-        lax.fori_loop(0, 4, body, 0)
-
-    def first(a):
-        for h in range(2):
-            pltpu.make_async_copy(srcs[a].at[pl.ds(h * half, half)], buf.at[h], lsem.at[h]).start()
-        for h in range(2):
-            recv(a, mate, h)
-            pltpu.make_async_copy(view(a, mate, h), buf.at[2 + h], lsem.at[2 + h]).start()
-        project(a, me, 0, me, 1)
-        outs = [pltpu.make_async_copy(buf.at[h], view(a, me, h), osem.at[h]) for h in range(2)]
-        for c in outs:
-            c.start()
-        for c in outs:
-            c.wait()
-
-    def event(a, e):
-        b0, h0, b1, h1 = ((left, 0, right, 1), (left, 1, right, 0), (opp, 0, opp, 1))[e - 1]
-        recv(a, b0, h0)
-        if e == 1:
-            send(view(a, b0, h0), a, b0, h0, ssem_r.at[a, 2], right)
-        send(view(a, b0, h0), a, b0, h0, ssem_p.at[a, 2 * e], mate)
-        pltpu.make_async_copy(view(a, b0, h0), buf.at[0], lsem.at[0]).start()
-        recv(a, b1, h1)
-        if e == 1:
-            send(view(a, b1, h1), a, b1, h1, ssem_l.at[a, 2], left)
-        send(view(a, b1, h1), a, b1, h1, ssem_p.at[a, 2 * e + 1], mate)
-        pltpu.make_async_copy(view(a, b1, h1), buf.at[1], lsem.at[1]).start()
-        for i, (b, h) in enumerate(((b0, h0), (b1, h1))):
-            recv(a, b + flip, h)
-            pltpu.make_async_copy(view(a, b + flip, h), buf.at[2 + i], lsem.at[2 + i]).start()
-        project(a, b0, h0, b1, h1)
-
-    first(0)
-    first(1)
-    for a, e in ((0, 1), (0, 2), (1, 1), (1, 2), (0, 3), (1, 3)):
-        event(a, e)
-    for c in sends:
-        c.wait_send()
-
-
-def _grad_kernel(n, scale, q, k, v, do, xf, dyf, wq, wk, wv,
-                 dx, dwq, dwo, dwk, dwv, wqf,
-                 s_ref, p_ref, acc, lhs, dqs, dqr, kvr, kvx, dwr, dwx, xbuf,
-                 mrow, lrow, oacc, qt, dot_,
-                 w_sr, w_sl, w_sp, w_recv, dq_send, dq_recv, kv_send, kv_recv,
-                 rs_send, rs_recv, x_sem, b_sem):
+def _kernel(n, scale, x, dy, wq, wk, wv, wo,
+            dx, dwq, dwo, dwk, dwv, xf, dyf, wqf,
+            q, k, v, do, wq_v, wk_v, wv_v, wo_v,
+            s_ref, p_ref, acc, lhs, dqs, dqr, kvr, kvx, dwr, dwx, xbuf,
+            mrow, lrow, oacc, qt, dot_, dwo_v, stage,
+            g_sr, g_sl, g_sp, g_recv, l_sem,
+            w_sr, w_sl, w_sp, w_recv, dq_send, dq_recv, kv_send, kv_recv,
+            rs_send, rs_recv, x_sem, b_sem, o_sem):
     me, core, right, left, opp, mate = _ring(n)
     chip = me // 2
     flip = 1 - 2 * core
     blk, width = q.shape[1], q.shape[2]
-    model = dwq.shape[0]
+    half = blk // 2
+    model = x.shape[1]
     tile = model // (n // 2)
     lanes = 128
     whalf = model // 2
     _barrier([lax.rem(me + d, n) for d in range(1, n)])
     sends = []
 
+    srcs, dsts = (x, dy), (xf, dyf)
+
+    def view(a, b, h):
+        return dsts[a].at[b, pl.ds(h * half, half)]
+
+    def send(src, a, b, h, ssem, dev):
+        _remote(src, view(a, b, h), ssem, g_recv.at[a, b * 2 + h], dev).start()
+
+    def recv(a, b, h):
+        _remote(view(a, b, h), view(a, b, h), g_sp.at[a, 0], g_recv.at[a, b * 2 + h], mate).wait_recv()
+
+    def own(a, h):
+        return srcs[a].at[pl.ds(h * half, half)]
+
+    def send_own(a):
+        for i, h in enumerate((0, 1)):
+            send(own(a, h), a, me, h, g_sr.at[a, i], right)
+            send(own(a, 1 - h), a, me, 1 - h, g_sl.at[a, i], left)
+
+    def chunk(i):
+        return xbuf.at[i // 2, pl.ds(lax.rem(i, 2) * half, half)]
+
+    def load(src, i):
+        return pltpu.make_async_copy(src, chunk(i), l_sem.at[i])
+
+    def project(a, b0, h0, b1, h1):
+        def body(i, carry):
+            side, par = lax.rem(i, 2), i // 2
+            b = b0 + side * (b1 - b0) + par * flip
+            h = h0 + side * (h1 - h0)
+            load(view(a, b, h), i).wait()
+            at = pl.ds(pl.multiple_of(h * half, half), half)
+            data = chunk(i)[...]
+            if a == 0:
+                q[b, at] = _mm(data, wq_v[...]).astype(BF16)
+                k[b, at] = _mm(data, wk_v[...]).astype(BF16)
+                v[b, at] = _mm(data, wv_v[...]).astype(BF16)
+            else:
+                do[b, at] = _mm_t(data, wo_v[...]).astype(BF16)
+            return carry
+        lax.fori_loop(0, 4, body, 0)
+
+    def first(a):
+        for h in range(2):
+            load(own(a, h), h).start()
+        for h in range(2):
+            recv(a, mate, h)
+            load(view(a, mate, h), 2 + h).start()
+        project(a, me, 0, me, 1)
+
+    def event(a, e):
+        b0, h0, b1, h1 = ((left, 0, right, 1), (left, 1, right, 0), (opp, 0, opp, 1))[e - 1]
+        for i, (b, h) in enumerate(((b0, h0), (b1, h1))):
+            recv(a, b, h)
+            if e == 1:
+                send(view(a, b, h), a, b, h, (g_sr, g_sl)[i].at[a, 2], (right, left)[i])
+            send(view(a, b, h), a, b, h, g_sp.at[a, 2 * e + i], mate)
+            load(view(a, b, h), i).start()
+        if e == 1:
+            if a == 0:
+                send_own(1)
+            else:
+                send_wq()
+        for i, (b, h) in enumerate(((b0, h0), (b1, h1))):
+            recv(a, b + flip, h)
+            load(view(a, b + flip, h), 2 + i).start()
+        project(a, b0, h0, b1, h1)
+
     def wview(b, h):
         return wqf.at[b, pl.ds(h * whalf, whalf)]
 
@@ -158,11 +142,13 @@
     def wrecv(b, h):
         _remote(wview(b, h), wview(b, h), w_sp.at[0], w_recv.at[b * 2 + h], mate).wait_recv()
 
-    for i, h in enumerate((0, 1)):
-        wsend(wq.at[pl.ds(h * whalf, whalf)], me, h, w_sr.at[i], right)
-        wsend(wq.at[pl.ds((1 - h) * whalf, whalf)], me, 1 - h, w_sl.at[i], left)
-    for h in range(2):
-        wsend(wq.at[pl.ds(h * whalf, whalf)], me, h, w_sp.at[h], mate)
+    def wown(h):
+        return wq.at[pl.ds(h * whalf, whalf)]
+
+    def send_wq():
+        for i, h in enumerate((0, 1)):
+            wsend(wown(h), me, h, w_sr.at[i], right)
+            wsend(wown(1 - h), me, 1 - h, w_sl.at[i], left)
 
     def wevent(e):
         b0, h0, b1, h1 = ((left, 0, right, 1), (left, 1, right, 0), (opp, 0, opp, 1))[e - 1]
@@ -174,8 +160,23 @@
         wsend(wview(b0, h0), b0, h0, w_sp.at[2 * e], mate)
         wsend(wview(b1, h1), b1, h1, w_sp.at[2 * e + 1], mate)
 
+    send_own(0)
+    for a in range(2):
+        for h in range(2):
+            send(own(a, h), a, me, h, g_sp.at[a, h], mate)
+    for h in range(2):
+        wsend(wown(h), me, h, w_sp.at[h], mate)
+    loads = [pltpu.make_async_copy(src, dst, o_sem.at[i])
+             for i, (src, dst) in enumerate(((wq, wq_v), (wk, wk_v), (wv, wv_v), (wo, wo_v)))]
+    for c in loads:
+        c.start()
     acc[...] = jnp.zeros_like(acc)
-    dwo[...] = jnp.zeros_like(dwo)
+    dwo_v[...] = jnp.zeros_like(dwo_v)
+    for c in loads:
+        c.wait()
+    first(0)
+    for e in (1, 2, 3):
+        event(0, e)
 
     def fold(val, op):
         out = val[:, :lanes]
@@ -184,9 +185,36 @@
         return out
 
     def q_step(t, carry):
-        nb = lax.rem(me + 1 + t, n)
+        p = t // 2
+        nb = lax.rem(me + 2 * p + 2 * (p // 2) * (1 - 2 * lax.rem(p, 2)), n) + lax.rem(t, 2) * flip
+
+        @pl.when(t == 0)
+        def _():
+            first(1)
+
+        @pl.when(t == 2)
+        def _():
+            event(1, 1)
+            event(1, 2)
+
+        @pl.when(t == 6)
+        def _():
+            event(1, 3)
+
+        @pl.when(t == 7)
+        def _():
+            wevent(1)
+
         dy_copy = pltpu.make_async_copy(dyf.at[nb], xbuf.at[0], x_sem.at[0])
-        dy_copy.start()
+
+        @pl.when(t == 0)
+        def _():
+            pltpu.make_async_copy(dy, xbuf.at[0], x_sem.at[0]).start()
+
+        @pl.when(t > 0)
+        def _():
+            dy_copy.start()
+
         qn = q[nb]
         don = do[nb]
         qt[...] = qn.T
@@ -245,27 +273,19 @@
         dqs[nb] = dq
         lhs[nb, 0:width] = dq.T
 
-        @pl.when(t < n - 1)
+        @pl.when(t > 0)
         def _():
             _remote(dqs.at[nb], dqr.at[me], dq_send.at[nb], dq_recv.at[me], nb).start()
 
-        @pl.when(t == n - 1)
+        @pl.when(t == 0)
         def _():
             dqr[me] = dq
-
-        @pl.when(t == 3)
-        def _():
-            wevent(1)
-
-        @pl.when(t == 5)
-        def _():
-            wevent(2)
 
         dy_copy.wait()
         ot = ob.T
         for c in range(model // tile):
             at = pl.ds(c * tile, tile)
-            dwo[:, at] += _mm(ot, xbuf[0, :, at])
+            dwo_v[:, at] += _mm(ot, xbuf[0, :, at])
         return carry
 
     lax.fori_loop(0, n, q_step, 0)
@@ -286,6 +306,8 @@
 
     lax.fori_loop(0, n, convert, 0)
 
+    out_wo = pltpu.make_async_copy(dwo_v, dwo, o_sem.at[0])
+    out_wo.start()
     half_chips = n // 2
 
     def stag(b):
@@ -325,15 +347,17 @@
     def x_copy(b, slot):
         return pltpu.make_async_copy(xf.at[b], xbuf.at[slot], x_sem.at[slot])
 
-    x_copy(0, 0).start()
-
-    def x_step(b, carry):
-        slot = lax.rem(b, 2)
+    pltpu.make_async_copy(x, xbuf.at[0], x_sem.at[0]).start()
+    wevent(2)
+
+    def x_step(i, carry):
+        slot = lax.rem(i, 2)
+        b = lax.rem(me + i, n)
         x_copy(b, slot).wait()
 
-        @pl.when(b < n - 1)
-        def _():
-            x_copy(b + 1, 1 - slot).start()
+        @pl.when(i < n - 1)
+        def _():
+            x_copy(lax.rem(me + i + 1, n), 1 - slot).start()
 
         for c in range(model // tile):
             xt = xbuf[slot, :, c * tile:(c + 1) * tile]
@@ -414,7 +438,9 @@
     rs_start(acc.at[1, lb // 2, :, pl.ds(tile // 2, tile // 2)], dwr, 1, 1, 1)
 
     for c in range(model // tile):
-        dwq[c * tile:(c + 1) * tile] = acc[0, c].T
+        for g in range(2):
+            stage[c, pl.ds(g, tile, stride=2)] = acc[0, c, g * lanes:(g + 1) * lanes].T
+        pltpu.make_async_copy(stage.at[c], dwq.at[pl.ds(c * 2 * tile, 2 * tile)], l_sem.at[c]).start()
 
     rs_wait(kvr, 0, 0, 1)
     rs_wait(kvr, 0, 1, 2)
@@ -445,11 +471,14 @@
     for c in range(model // tile):
         at = slice(c * tile, (c + 1) * tile)
         total = s_ref[c]
-        for i, w in enumerate((wk, wv)):
+        for i, w in enumerate((wk_v, wv_v)):
             wt = w[at]
             total += (_mm_t(dqs[3 * i + 2], wt) + _mm_t(dqs[3 * i + 1], wt)) + _mm_t(dqs[3 * i], wt)
-        dx[:, at] = total.astype(BF16)
-
+        xbuf[0, :, at] = total.astype(BF16)
+    out_dx = pltpu.make_async_copy(xbuf.at[0], dx, x_sem.at[0])
+    out_dx.start()
+
+    outs = [out_wo, out_dx]
     rs_wait(dwr, 1, 0, 1)
     rs_wait(dwr, 1, 1, 2)
     acc[1, base // 2, :, part_cols(0)] += dwr[0, 1] + dwr[1, 2]
@@ -460,11 +489,23 @@
     swap.start()
     dwx[1] = part(me)[...]
     swap.wait()
-    dwk[...] = dwx[1 - core].T
-    dwv[...] = dwx[core].T
+    for i, (val, out) in enumerate(((dwx[1 - core].T, dwk), (dwx[core].T, dwv))):
+        oacc[i * width:(i + 1) * width] = val
+        outs.append(pltpu.make_async_copy(oacc.at[pl.ds(i * width, width)], out, o_sem.at[1 + i]))
+        outs[-1].start()
+    for c in outs:
+        c.wait()
+    for c in range(model // tile):
+        pltpu.make_async_copy(stage.at[c], dwq.at[pl.ds(c * 2 * tile, 2 * tile)], l_sem.at[c]).wait()
 
     for c in sends:
         c.wait_send()
+    for a in range(2):
+        for i in range(3):
+            _remote(view(a, me, 0), view(a, me, 0), g_sr.at[a, i], g_recv.at[a, 0], mate).wait_send()
+            _remote(view(a, me, 0), view(a, me, 0), g_sl.at[a, i], g_recv.at[a, 0], mate).wait_send()
+        for i in range(8):
+            _remote(view(a, me, 0), view(a, me, 0), g_sp.at[a, i], g_recv.at[a, 0], mate).wait_send()
     for i in range(3):
         _remote(wview(me, 0), wview(me, 0), w_sr.at[i], w_recv.at[0], mate).wait_send()
         _remote(wview(me, 0), wview(me, 0), w_sl.at[i], w_recv.at[0], mate).wait_send()
@@ -474,7 +515,6 @@
 
 def solution(mesh):
     n = mesh.shape["tp"]
-    vmem = pl.BlockSpec(memory_space=pltpu.VMEM)
     hbm = pl.BlockSpec(memory_space=pl.ANY)
     dma = pltpu.SemaphoreType.DMA
 
@@ -486,37 +526,29 @@
         wk2 = w_k.reshape(model, width)
         wv2 = w_v.reshape(model, width)
         wo2 = wo_loc.reshape(width, model)
+        tile = 2 * model // n
         full = jax.ShapeDtypeStruct((n, rows, model), BF16)
-        proj = jax.ShapeDtypeStruct((n * rows, width), BF16)
-        xf, dyf, q, k, v, do = pl.pallas_call(
-            functools.partial(_gather_kernel, n),
-            name="gather_project",
-            out_shape=(full, full, proj, proj, proj, proj),
-            in_specs=[hbm, hbm, vmem, vmem, vmem, vmem],
-            out_specs=(hbm, hbm, vmem, vmem, vmem, vmem),
-            scratch_shapes=[
-                pltpu.VMEM((4, rows // 2, model), BF16),
-                dma((2, 3)), dma((2, 3)), dma((2, 8)), dma((2, 2 * n)), dma((4,)), dma((2,)),
-            ],
-            compiler_params=pltpu.CompilerParams(
-                collective_id=0, has_side_effects=True, vmem_limit_bytes=32 * 2 ** 20),
-        )(x_blk, dy_blk, wq2, wk2, wv2, wo2)
-        q, k, v, do = (a.reshape(n, rows, width) for a in (q, k, v, do))
-        tile = 2 * model // n
-        dx, dwq, dwo, dwk, dwv, _ = pl.pallas_call(
-            functools.partial(_grad_kernel, n, scale),
+        proj = pltpu.VMEM((n, rows, width), BF16)
+        dx, dwq, dwo, dwk, dwv, _, _, _ = pl.pallas_call(
+            functools.partial(_kernel, n, scale),
             name="attention_grads",
             out_shape=(
                 jax.ShapeDtypeStruct((rows, model), BF16),
-                jax.ShapeDtypeStruct((model, width), F32),
+                jax.ShapeDtypeStruct((2 * model, 128), F32),
                 jax.ShapeDtypeStruct((width, model), F32),
                 jax.ShapeDtypeStruct((model // n, width), F32),
                 jax.ShapeDtypeStruct((model // n, width), F32),
+                full, full,
                 jax.ShapeDtypeStruct((n, model, width), BF16),
             ),
-            in_specs=[vmem] * 4 + [hbm] * 3 + [vmem] * 2,
-            out_specs=(vmem,) * 5 + (hbm,),
+            in_specs=[hbm] * 6,
+            out_specs=(hbm,) * 8,
             scratch_shapes=[
+                proj, proj, proj, proj,
+                pltpu.VMEM((model, width), BF16),
+                pltpu.VMEM((model, width), BF16),
+                pltpu.VMEM((model, width), BF16),
+                pltpu.VMEM((width, model), BF16),
                 pltpu.VMEM((n, rows, rows), F32),
                 pltpu.VMEM((n, rows, rows), BF16),
                 pltpu.VMEM((2, n, width, rows), F32),
@@ -533,13 +565,16 @@
                 pltpu.VMEM((rows, width), F32),
                 pltpu.VMEM((width, rows), BF16),
                 pltpu.VMEM((width, rows), BF16),
+                pltpu.VMEM((width, model), F32),
+                pltpu.VMEM((n // 2, 2 * tile, 128), F32),
+                dma((2, 3)), dma((2, 3)), dma((2, 8)), dma((2, 2 * n)), dma((4,)),
                 dma((3,)), dma((3,)), dma((8,)), dma((2 * n,)),
                 dma((n,)), dma((n,)), dma((n,)), dma((n,)),
-                dma((2, 2, 3)), dma((2, 2, 3)), dma((2,)), dma((3, n)),
+                dma((2, 2, 3)), dma((2, 2, 3)), dma((2,)), dma((3, n)), dma((4,)),
             ],
             compiler_params=pltpu.CompilerParams(
-                collective_id=1, has_side_effects=True, vmem_limit_bytes=VMEM_MAX),
-        )(q, k, v, do, xf, dyf, wq2, wk2, wv2)
+                collective_id=0, has_side_effects=True, vmem_limit_bytes=VMEM_MAX),
+        )(x_blk, dy_blk, wq2, wk2, wv2, wo2)
         return (dx, dwq.reshape(model, 1, width), dwo.reshape(1, width, model), dwk, dwv)
 
     tok_spec = P(("dp", "tp"))

time: 312 us -> 271 us (0.87)
  Pallas kernels: 287 us -> 260 us
  local copies, waits for them, and re-layouts: 23.4 us -> 8.39 us
    pallas_call x2 -> x1, Pallas kernels: 287 us -> 260 us  [local_grads(): pl.pallas_call(functools.partial(_kernel, n, scale), name='attention_grad...]
    unnamed x33 -> x13, local copies, waits for them, and re-layouts: 23.4 us -> 8.39 us
where the time goes in v2:
time: 271 us; the launch traced here: 269 us
  Pallas kernels  260 us (96%)
  local copies, waits for them, and re-layouts  8.39 us (3%)
    pallas_call x1, Pallas kernels, local_grads(): pl.pallas_call(functools.partial(_kernel, n, scale), name='attention_grad...  260 us
    unnamed x13, local copies, waits for them, and re-layouts  8.39 us

profile of v2, /device:TPU:113, one launch (start us, length us, event | category | flops | bytes accessed | tf_op | source)
XLA Modules:
  0.0 269.4 jit_solution(7197402975265676192)
XLA Ops:
  0.6 260.3 %attention_grads.1 = (bf16[512,2048]{1,0:T(8,128)(2,1)}, f32[4096,128]{1,0:T(8,128)}, f32[256,2048]{1,0:T(8,128)}, f32[256,256]{1,0:T(8,128)}, f32[256,256]{1,0:...) custom-call(bf16[512,2048]{1,0:T(8,128)(2,1)} %x.1, ...), custom_call_target="tpu_custom_call" | custom-call | tf_op jit(solution)/shard_map/attention_grads/pallas_call | solution.py:532
  261.0 0.0 copy-start.1
  261.0 3.3 %copy.17 = bf16[512,2048]{1,0:T(8,128)(2,1)} copy(bf16[512,2048]{1,0:T(8,128)(2,1)} %get-tuple-element.25) | data formatting | bytes 4194304
  264.3 0.0 copy-done.1
  264.3 0.0 copy-start
  264.3 1.3 copy.18
  265.6 1.0 copy-done
  266.6 0.0 copy-start.3
  266.6 0.0 copy-start.2
  266.6 1.3 copy.19
  267.9 0.0 copy-done.3
  268.0 0.7 copy.20
  268.7 0.0 copy-done.2
  268.7 0.7 copy.21
Async XLA Ops:
  261.0 3.3 %copy-start.1 = (f32[4096,128]{1,0:T(8,128)S(1)}, f32[4096,128]{1,0:T(8,128)}, u32[]{:S(2)}) copy-start(f32[4096,128]{1,0:T(8,128)} %get-tuple-element.11) | copy-start | bytes 6291460
  264.3 2.3 copy-start
  266.6 1.3 copy-start.3
  266.6 2.0 copy-start.2

commit v3 on v2

--- a/solution.py
+++ b/solution.py
@@ -48,8 +48,8 @@
 def _kernel(n, scale, x, dy, wq, wk, wv, wo,
             dx, dwq, dwo, dwk, dwv, xf, dyf, wqf,
             q, k, v, do, wq_v, wk_v, wv_v, wo_v,
-            s_ref, p_ref, acc, lhs, dqs, dqr, kvr, kvx, dwr, dwx, xbuf,
-            mrow, lrow, oacc, qt, dot_, dwo_v, stage,
+            s_ref, p_ref, acc, lhs, o, lse, dqr, kvr, kvx, dwr, dwx, xbuf,
+            mrow, lrow, oacc, qt, dot_, dwo_v,
             g_sr, g_sl, g_sp, g_recv, l_sem,
             w_sr, w_sl, w_sp, w_recv, dq_send, dq_recv, kv_send, kv_recv,
             rs_send, rs_recv, x_sem, b_sem, o_sem):
@@ -184,6 +184,52 @@
             out = op(out, val[:, c * lanes:(c + 1) * lanes])
         return out
 
+    def groups(val):
+        return [val[:, c * lanes:(c + 1) * lanes] for c in range(val.shape[1] // lanes)]
+
+    def expo(val, top):
+        return jnp.exp2((val - top) * (scale * LOG2E))
+
+    keep = (lax.broadcasted_iota(jnp.int32, (blk, blk), 0)
+            >= lax.broadcasted_iota(jnp.int32, (blk, blk), 1))
+
+    def forward(nb, carry):
+        mrow[...] = jnp.full_like(mrow, jnp.finfo(F32).min)
+        lrow[...] = jnp.zeros_like(lrow)
+
+        def stats(j, sc):
+            s_ref[j] = sc
+            old = mrow[...]
+            top = jnp.maximum(old, fold(sc, jnp.maximum))
+            total = lrow[...] * expo(old, top)
+            for part in groups(sc):
+                total += expo(part, top)
+            mrow[...] = top
+            lrow[...] = total
+
+        def scores(j, carry):
+            stats(j, _mm_t(q[nb], k[j]))
+            return carry
+
+        lax.fori_loop(0, nb, scores, 0)
+        stats(nb, jnp.where(keep, _mm_t(q[nb], k[nb]), -jnp.inf))
+        top = jnp.max(mrow[...], axis=1, keepdims=True)
+        total = jnp.sum(lrow[...] * expo(mrow[...], top), axis=1, keepdims=True)
+        lse[nb] = jnp.broadcast_to(top + jnp.log(total) * (1.0 / scale), mrow.shape)
+        oacc[...] = jnp.zeros_like(oacc)
+
+        def values(j, carry):
+            shift = lse[nb]
+            pb = jnp.concatenate([expo(part, shift).astype(BF16) for part in groups(s_ref[j])], axis=1)
+            oacc[...] += _mm(pb, v[j])
+            return carry
+
+        lax.fori_loop(0, nb + 1, values, 0)
+        o[nb] = oacc[...].astype(BF16)
+        return carry
+
+    lax.fori_loop(0, n, forward, 0)
+
     def q_step(t, carry):
         p = t // 2
         nb = lax.rem(me + 2 * p + 2 * (p // 2) * (1 - 2 * lax.rem(p, 2)), n) + lax.rem(t, 2) * flip
@@ -191,10 +237,10 @@
         @pl.when(t == 0)
         def _():
             first(1)
+            event(1, 1)
 
         @pl.when(t == 2)
         def _():
-            event(1, 1)
             event(1, 2)
 
         @pl.when(t == 6)
@@ -215,74 +261,45 @@
         def _():
             dy_copy.start()
 
-        qn = q[nb]
-        don = do[nb]
-        qt[...] = qn.T
-        dot_[...] = don.T
-        mrow[...] = jnp.full_like(mrow, -jnp.inf)
-
-        def scores(j, _):
-            sc = _mm_t(q[nb], k[j])
-            s_ref[j] = sc
-            mrow[...] = jnp.maximum(mrow[...], fold(sc, jnp.maximum))
-            return _
-
-        lax.fori_loop(0, nb, scores, 0)
-        sc = _mm_t(qn, k[nb])
-        keep = (lax.broadcasted_iota(jnp.int32, sc.shape, 0)
-                >= lax.broadcasted_iota(jnp.int32, sc.shape, 1))
-        sc = jnp.where(keep, sc, -jnp.inf)
-        s_ref[nb] = sc
-        m = jnp.max(jnp.maximum(mrow[...], fold(sc, jnp.maximum)), axis=1, keepdims=True)
-        mrow[...] = jnp.broadcast_to(m, mrow.shape)
-        lrow[...] = jnp.zeros_like(lrow)
-
-        def expo(j, _):
-            pr = jnp.exp2((s_ref[j] - mrow[:, :1]) * (scale * LOG2E))
-            s_ref[j] = pr
-            lrow[...] += fold(pr, jnp.add)
-            return _
-
-        lax.fori_loop(0, nb + 1, expo, 0)
-        inv = 1.0 / jnp.sum(lrow[...], axis=1, keepdims=True)
-        lrow[...] = jnp.broadcast_to(inv, lrow.shape)
-        oacc[...] = jnp.zeros_like(oacc)
-
-        def values(j, _):
-            pb = (s_ref[j] * lrow[:, :1]).astype(BF16)
-            p_ref[j] = pb
-            oacc[...] += _mm(pb, v[j])
-            return _
-
-        lax.fori_loop(0, nb + 1, values, 0)
-        ob = oacc[...].astype(BF16)
-        delta = jnp.sum(don.astype(F32) * ob.astype(F32), axis=1, keepdims=True)
+        qt[...] = q[nb].T
+        dot_[...] = do[nb].T
+        delta = jnp.sum(do[nb].astype(F32) * o[nb].astype(F32), axis=1, keepdims=True)
         mrow[...] = jnp.broadcast_to(delta, mrow.shape)
         oacc[...] = jnp.zeros_like(oacc)
 
-        def grads(j, _):
-            dp = _mm_t(do[nb], v[j])
-            ds = (s_ref[j] * lrow[:, :1] * (dp - mrow[:, :1])).astype(BF16)
+        def grads(j, mask):
+            sc = groups(_mm_t(q[nb], k[j]))
+            dp = groups(_mm_t(do[nb], v[j]))
+            shift, less = lse[nb], mrow[...]
+            pr = [expo(part, shift) for part in sc]
+            if mask:
+                pr = [jnp.where(kg, part, 0.0) for kg, part in zip(groups(keep), pr)]
+            ds = jnp.concatenate([(pp * (dd - less)).astype(BF16) for pp, dd in zip(pr, dp)], axis=1)
+            pb = jnp.concatenate([pp.astype(BF16) for pp in pr], axis=1)
             oacc[...] += _mm(ds, k[j])
             acc[0, j] += _mm(qt[...], ds)
-            acc[1, j] += _mm(dot_[...], p_ref[j])
-            return _
-
-        lax.fori_loop(0, nb + 1, grads, 0)
+            acc[1, j] += _mm(dot_[...], pb)
+
+        def below(j, carry):
+            grads(j, False)
+            return carry
+
+        lax.fori_loop(0, nb, below, 0)
+        grads(nb, True)
         dq = (oacc[...] * scale).astype(BF16)
-        dqs[nb] = dq
+        q[nb] = dq
         lhs[nb, 0:width] = dq.T
 
         @pl.when(t > 0)
         def _():
-            _remote(dqs.at[nb], dqr.at[me], dq_send.at[nb], dq_recv.at[me], nb).start()
+            _remote(q.at[nb], dqr.at[me], dq_send.at[nb], dq_recv.at[me], nb).start()
 
         @pl.when(t == 0)
         def _():
             dqr[me] = dq
 
         dy_copy.wait()
-        ot = ob.T
+        ot = o[nb].T
         for c in range(model // tile):
             at = pl.ds(c * tile, tile)
             dwo_v[:, at] += _mm(ot, xbuf[0, :, at])
@@ -437,10 +454,14 @@
     acc[1, lb // 2, :, part_cols(1)] += dwr[1, 0]
     rs_start(acc.at[1, lb // 2, :, pl.ds(tile // 2, tile // 2)], dwr, 1, 1, 1)
 
+    def q_copy(c):
+        return pltpu.make_async_copy(lse.at[pl.ds(2 * c, 2)], dwq.at[pl.ds(2 * c, 2)], l_sem.at[c])
+
     for c in range(model // tile):
-        for g in range(2):
-            stage[c, pl.ds(g, tile, stride=2)] = acc[0, c, g * lanes:(g + 1) * lanes].T
-        pltpu.make_async_copy(stage.at[c], dwq.at[pl.ds(c * 2 * tile, 2 * tile)], l_sem.at[c]).start()
+        for g in range(4):
+            lse[2 * c + g // 2, pl.ds(g % 2, half, stride=2)] = (
+                acc[0, c, (g % 2) * lanes:(g % 2 + 1) * lanes, (g // 2) * half:(g // 2 + 1) * half].T)
+        q_copy(c).start()
 
     rs_wait(kvr, 0, 0, 1)
     rs_wait(kvr, 0, 1, 2)
@@ -467,13 +488,13 @@
         _remote(dqr.at[peer], dqr.at[peer], dq_send.at[peer], dq_recv.at[peer], peer).wait_send()
     for i, parts in enumerate((split(kv_first), split(kv_second))):
         for g, val in enumerate(parts):
-            dqs[3 * i + g] = val
+            q[3 * i + g] = val
     for c in range(model // tile):
         at = slice(c * tile, (c + 1) * tile)
         total = s_ref[c]
         for i, w in enumerate((wk_v, wv_v)):
             wt = w[at]
-            total += (_mm_t(dqs[3 * i + 2], wt) + _mm_t(dqs[3 * i + 1], wt)) + _mm_t(dqs[3 * i], wt)
+            total += (_mm_t(q[3 * i + 2], wt) + _mm_t(q[3 * i + 1], wt)) + _mm_t(q[3 * i], wt)
         xbuf[0, :, at] = total.astype(BF16)
     out_dx = pltpu.make_async_copy(xbuf.at[0], dx, x_sem.at[0])
     out_dx.start()
@@ -496,7 +517,7 @@
     for c in outs:
         c.wait()
     for c in range(model // tile):
-        pltpu.make_async_copy(stage.at[c], dwq.at[pl.ds(c * 2 * tile, 2 * tile)], l_sem.at[c]).wait()
+        q_copy(c).wait()
 
     for c in sends:
         c.wait_send()
@@ -534,7 +555,7 @@
             name="attention_grads",
             out_shape=(
                 jax.ShapeDtypeStruct((rows, model), BF16),
-                jax.ShapeDtypeStruct((2 * model, 128), F32),
+                jax.ShapeDtypeStruct((n, rows, 128), F32),
                 jax.ShapeDtypeStruct((width, model), F32),
                 jax.ShapeDtypeStruct((model // n, width), F32),
                 jax.ShapeDtypeStruct((model // n, width), F32),
@@ -554,6 +575,7 @@
                 pltpu.VMEM((2, n, width, rows), F32),
                 pltpu.VMEM((n, 3 * width, rows), BF16),
                 pltpu.VMEM((n, rows, width), BF16),
+                pltpu.VMEM((n, rows, 128), F32),
                 pltpu.VMEM((n, rows, width), BF16),
                 pltpu.VMEM((2, 3, width, rows), F32),
                 pltpu.VMEM((2, width, rows), F32),
@@ -566,7 +588,6 @@
                 pltpu.VMEM((width, rows), BF16),
                 pltpu.VMEM((width, rows), BF16),
                 pltpu.VMEM((width, model), F32),
-                pltpu.VMEM((n // 2, 2 * tile, 128), F32),
                 dma((2, 3)), dma((2, 3)), dma((2, 8)), dma((2, 2 * n)), dma((4,)),
                 dma((3,)), dma((3,)), dma((8,)), dma((2 * n,)),
                 dma((n,)), dma((n,)), dma((n,)), dma((n,)),

time: 271 us -> 261 us (0.963)
  Pallas kernels: 260 us -> 252 us
    pallas_call x1, Pallas kernels: 260 us -> 252 us  [local_grads(): pl.pallas_call(functools.partial(_kernel, n, scale), name='attention_grad...]
where the time goes in v3:
time: 261 us
  Pallas kernels  252 us (97%)
  local copies, waits for them, and re-layouts  8.39 us (3%)
    pallas_call x1, Pallas kernels, local_grads(): pl.pallas_call(functools.partial(_kernel, n, scale), name='attention_grad...  252 us
    unnamed x13, local copies, waits for them, and re-layouts  8.39 us

profile of v3, /device:TPU:113, one launch (start us, length us, event | category | flops | bytes accessed | tf_op | source)
XLA Modules:
  0.0 261.2 jit_solution(10779212103577882591)
XLA Ops:
  0.6 252.1 %attention_grads.1 = (bf16[512,2048]{1,0:T(8,128)(2,1)}, f32[8,512,128]{2,1,0:T(8,128)}, f32[256,2048]{1,0:T(8,128)}, f32[256,256]{1,0:T(8,128)}, f32[256,256]{1...) custom-call(bf16[512,2048]{1,0:T(8,128)(2,1)} %x.1, ...), custom_call_target="tpu_custom_call" | custom-call | tf_op jit(solution)/shard_map/attention_grads/pallas_call | solution.py:553
  252.8 0.0 copy-start.1
  252.8 3.3 %copy.17 = bf16[512,2048]{1,0:T(8,128)(2,1)} copy(bf16[512,2048]{1,0:T(8,128)(2,1)} %get-tuple-element.25) | data formatting | bytes 4194304
  256.1 0.0 copy-done.1
  256.1 0.0 copy-start
  256.1 1.3 copy.18
  257.4 1.0 copy-done
  258.4 0.0 copy-start.3
  258.5 0.0 copy-start.2
  258.5 1.3 copy.19
  259.8 0.0 copy-done.3
  259.8 0.7 copy.20
  260.5 0.0 copy-done.2
  260.5 0.7 copy.21
Async XLA Ops:
  252.8 3.3 %copy-start.1 = (f32[8,512,128]{2,1,0:T(8,128)S(1)}, f32[8,512,128]{2,1,0:T(8,128)}, u32[]{:S(2)}) copy-start(f32[8,512,128]{2,1,0:T(8,128)} %get-tuple-element.11) | copy-start | bytes 6291460
  256.1 2.3 copy-start
  258.4 1.3 copy-start.3
  258.5 2.0 copy-start.2

commit v4 on v3

--- a/solution.py
+++ b/solution.py
@@ -35,7 +35,7 @@
 def _barrier(devices):
     barrier = pltpu.get_barrier_semaphore()
     for d in devices:
-        pl.semaphore_signal(barrier, inc=1, device_id={"tp": d}, device_id_type=MESH)
+        pl.semaphore_signal(barrier, inc=1, device_id=d, device_id_type=MESH)
     pl.semaphore_wait(barrier, len(devices))
 
 
@@ -51,7 +51,7 @@
             s_ref, p_ref, acc, lhs, o, lse, dqr, kvr, kvx, dwr, dwx, xbuf,
             mrow, lrow, oacc, qt, dot_, dwo_v,
             g_sr, g_sl, g_sp, g_recv, l_sem,
-            w_sr, w_sl, w_sp, w_recv, dq_send, dq_recv, kv_send, kv_recv,
+            w_sr, w_sl, w_sp, w_st, w_recv, dq_send, dq_recv, kv_send, kv_recv,
             rs_send, rs_recv, x_sem, b_sem, o_sem):
     me, core, right, left, opp, mate = _ring(n)
     chip = me // 2
@@ -61,8 +61,10 @@
     model = x.shape[1]
     tile = model // (n // 2)
     lanes = 128
-    whalf = model // 2
-    _barrier([lax.rem(me + d, n) for d in range(1, n)])
+    group = lax.axis_index("dp")
+    side = lax.rem(group, 2)
+    twin = {"dp": group + 1 - 2 * side, "tp": me}
+    _barrier([{"tp": lax.rem(me + d, n)} for d in range(1, n)] + [twin])
     sends = []
 
     srcs, dsts = (x, dy), (xf, dyf)
@@ -133,39 +135,52 @@
             load(view(a, b + flip, h), 2 + i).start()
         project(a, b0, h0, b1, h1)
 
-    def wview(b, h):
-        return wqf.at[b, pl.ds(h * whalf, whalf)]
-
-    def wsend(src, b, h, ssem, dev):
-        _remote(src, wview(b, h), ssem, w_recv.at[b * 2 + h], dev).start()
-
-    def wrecv(b, h):
-        _remote(wview(b, h), wview(b, h), w_sp.at[0], w_recv.at[b * 2 + h], mate).wait_recv()
-
-    def wown(h):
-        return wq.at[pl.ds(h * whalf, whalf)]
+    quarter = model // 4
+
+    def wview(b, i):
+        return wqf.at[b, pl.ds(i * quarter, quarter)]
+
+    def wcopy(src, b, i, ssem, dev):
+        dev = dev if isinstance(dev, dict) else {"tp": dev}
+        return pltpu.make_async_remote_copy(
+            src_ref=src, dst_ref=wview(b, i), send_sem=ssem, recv_sem=w_recv.at[b, i],
+            device_id=dev, device_id_type=MESH)
+
+    def wrecv(b, i):
+        wcopy(wview(b, i), b, i, w_sp.at[0], mate).wait_recv()
+
+    def wown(i):
+        return wq.at[pl.ds(i * quarter, quarter)]
+
+    mine, other = 2 * side, 2 - 2 * side
 
     def send_wq():
-        for i, h in enumerate((0, 1)):
-            wsend(wown(h), me, h, w_sr.at[i], right)
-            wsend(wown(1 - h), me, 1 - h, w_sl.at[i], left)
+        for i in range(2):
+            wcopy(wown(mine + i), me, mine + i, w_sr.at[i], right).start()
+            wcopy(wown(mine + 1 - i), me, mine + 1 - i, w_sl.at[i], left).start()
 
     def wevent(e):
-        b0, h0, b1, h1 = ((left, 0, right, 1), (left, 1, right, 0), (opp, 0, opp, 1))[e - 1]
-        wrecv(b0, h0)
-        wrecv(b1, h1)
-        if e == 1:
-            wsend(wview(b0, h0), b0, h0, w_sr.at[2], right)
-            wsend(wview(b1, h1), b1, h1, w_sl.at[2], left)
-        wsend(wview(b0, h0), b0, h0, w_sp.at[2 * e], mate)
-        wsend(wview(b1, h1), b1, h1, w_sp.at[2 * e + 1], mate)
+        pieces = (((left, 0), (right, 1)), ((left, 1), (right, 0)), ((opp, 0), (opp, 1)))[e - 1]
+        for g, (b, i) in enumerate(pieces):
+            i = mine + i
+            wrecv(b, i)
+            if e == 1:
+                wcopy(wview(b, i), b, i, (w_sr, w_sl)[g].at[2], (right, left)[g]).start()
+            wcopy(wview(b, i), b, i, w_sp.at[2 + 2 * e + g], mate).start()
+            wcopy(wview(b, i), b, i, w_st.at[2 * e - 2 + g], twin).start()
+
+    def wtwin():
+        for g, (b, i) in enumerate(((left, 0), (right, 1), (left, 1), (right, 0), (opp, 0), (opp, 1))):
+            i = other + i
+            wrecv(b, i)
+            wcopy(wview(b, i), b, i, w_sp.at[10 + g], mate).start()
 
     send_own(0)
     for a in range(2):
         for h in range(2):
             send(own(a, h), a, me, h, g_sp.at[a, h], mate)
-    for h in range(2):
-        wsend(wown(h), me, h, w_sp.at[h], mate)
+    for i in range(4):
+        wcopy(wown(i), me, i, w_sp.at[i], mate).start()
     loads = [pltpu.make_async_copy(src, dst, o_sem.at[i])
              for i, (src, dst) in enumerate(((wq, wq_v), (wk, wk_v), (wv, wv_v), (wo, wo_v)))]
     for c in loads:
@@ -411,10 +426,10 @@
 
     for b in range(n):
         kv_copy(b).wait_send()
-    for e, (b0, h0, b1, h1) in enumerate(((mate, 0, mate, 1), (left + flip, 0, right + flip, 1),
-                                          (left + flip, 1, right + flip, 0), (opp + flip, 0, opp + flip, 1))):
-        wrecv(b0, h0)
-        wrecv(b1, h1)
+    wtwin()
+    for b in (mate, left + flip, right + flip, opp + flip):
+        for i in range(4):
+            wrecv(b, i)
     for d in range(1, n):
         peer = lax.rem(me + d, n)
         _remote(dqr.at[peer], dqr.at[peer], dq_send.at[peer], dq_recv.at[peer], peer).wait_recv()
@@ -527,11 +542,9 @@
             _remote(view(a, me, 0), view(a, me, 0), g_sl.at[a, i], g_recv.at[a, 0], mate).wait_send()
         for i in range(8):
             _remote(view(a, me, 0), view(a, me, 0), g_sp.at[a, i], g_recv.at[a, 0], mate).wait_send()
-    for i in range(3):
-        _remote(wview(me, 0), wview(me, 0), w_sr.at[i], w_recv.at[0], mate).wait_send()
-        _remote(wview(me, 0), wview(me, 0), w_sl.at[i], w_recv.at[0], mate).wait_send()
-    for i in range(8):
-        _remote(wview(me, 0), wview(me, 0), w_sp.at[i], w_recv.at[0], mate).wait_send()
+    for sems, count in ((w_sr, 3), (w_sl, 3), (w_sp, 16), (w_st, 6)):
+        for i in range(count):
+            wcopy(wview(me, 0), me, 0, sems.at[i], mate).wait_send()
 
 
 def solution(mesh):
@@ -589,7 +602,7 @@
                 pltpu.VMEM((width, rows), BF16),
                 pltpu.VMEM((width, model), F32),
                 dma((2, 3)), dma((2, 3)), dma((2, 8)), dma((2, 2 * n)), dma((4,)),
-                dma((3,)), dma((3,)), dma((8,)), dma((2 * n,)),
+                dma((3,)), dma((3,)), dma((16,)), dma((6,)), dma((n, 4)),
                 dma((n,)), dma((n,)), dma((n,)), dma((n,)),
                 dma((2, 2, 3)), dma((2, 2, 3)), dma((2,)), dma((3, n)), dma((4,)),
             ],

time: 261 us -> 251 us (0.962)
  Pallas kernels: 252 us -> 242 us
    pallas_call x1, Pallas kernels: 252 us -> 242 us  [local_grads(): pl.pallas_call(functools.partial(_kernel, n, scale), name='attention_grad...]
where the time goes in v4:
time: 251 us
  Pallas kernels  242 us (96%)
  local copies, waits for them, and re-layouts  8.39 us (3%)
    pallas_call x1, Pallas kernels, local_grads(): pl.pallas_call(functools.partial(_kernel, n, scale), name='attention_grad...  242 us
    unnamed x13, local copies, waits for them, and re-layouts  8.39 us

profile of v4, /device:TPU:113, one launch (start us, length us, event | category | flops | bytes accessed | tf_op | source)
XLA Modules:
  0.0 251.1 jit_solution(7934254467769692836)
XLA Ops:
  0.6 242.0 %attention_grads.1 = (bf16[512,2048]{1,0:T(8,128)(2,1)}, f32[8,512,128]{2,1,0:T(8,128)}, f32[256,2048]{1,0:T(8,128)}, f32[256,256]{1,0:T(8,128)}, f32[256,256]{1...) custom-call(bf16[512,2048]{1,0:T(8,128)(2,1)} %x.1, ...), custom_call_target="tpu_custom_call" | custom-call | tf_op jit(solution)/shard_map/attention_grads/pallas_call | solution.py:566
  242.7 0.0 copy-start.1
  242.7 3.3 %copy.17 = bf16[512,2048]{1,0:T(8,128)(2,1)} copy(bf16[512,2048]{1,0:T(8,128)(2,1)} %get-tuple-element.25) | data formatting | bytes 4194304
  246.0 0.0 copy-done.1
  246.0 0.0 copy-start
  246.0 1.3 copy.18
  247.3 1.0 copy-done
  248.3 0.0 copy-start.3
  248.3 0.0 copy-start.2
  248.3 1.3 copy.19
  249.7 0.0 copy-done.3
  249.7 0.7 copy.20
  250.4 0.0 copy-done.2
  250.4 0.7 copy.21
Async XLA Ops:
  242.7 3.3 %copy-start.1 = (f32[8,512,128]{2,1,0:T(8,128)S(1)}, f32[8,512,128]{2,1,0:T(8,128)}, u32[]{:S(2)}) copy-start(f32[8,512,128]{2,1,0:T(8,128)} %get-tuple-element.11) | copy-start | bytes 6291460
  246.0 2.3 copy-start
  248.3 1.3 copy-start.3
  248.3 2.0 copy-start.2

commit v5 on v4

--- a/solution.py
+++ b/solution.py
@@ -49,7 +49,7 @@
             dx, dwq, dwo, dwk, dwv, xf, dyf, wqf,
             q, k, v, do, wq_v, wk_v, wv_v, wo_v,
             s_ref, p_ref, acc, lhs, o, lse, dqr, kvr, kvx, dwr, dwx, xbuf,
-            mrow, lrow, oacc, qt, dot_, dwo_v,
+            mrow, oacc, qt, dot_, dwo_v,
             g_sr, g_sl, g_sp, g_recv, l_sem,
             w_sr, w_sl, w_sp, w_st, w_recv, dq_send, dq_recv, kv_send, kv_recv,
             rs_send, rs_recv, x_sem, b_sem, o_sem):
@@ -189,9 +189,6 @@
     dwo_v[...] = jnp.zeros_like(dwo_v)
     for c in loads:
         c.wait()
-    first(0)
-    for e in (1, 2, 3):
-        event(0, e)
 
     def fold(val, op):
         out = val[:, :lanes]
@@ -208,46 +205,78 @@
     keep = (lax.broadcasted_iota(jnp.int32, (blk, blk), 0)
             >= lax.broadcasted_iota(jnp.int32, (blk, blk), 1))
 
+    def order(t):
+        p = t // 2
+        return lax.rem(me + 2 * p + 2 * (p // 2) * (1 - 2 * lax.rem(p, 2)), n) + lax.rem(t, 2) * flip
+
+    def stats(nb, j, mask):
+        sc = _mm_t(q[nb], k[j])
+        if mask:
+            sc = jnp.where(keep, sc, -jnp.inf)
+        old = lse[nb]
+        top = jnp.maximum(old, fold(sc, jnp.maximum))
+        total = s_ref[nb, :, 0:lanes] * expo(old, top)
+        for part in groups(sc):
+            total += expo(part, top)
+        lse[nb] = top
+        s_ref[nb, :, 0:lanes] = total
+
+    def land(t, carry):
+        @pl.when(t == 0)
+        def _():
+            first(0)
+
+        @pl.when(t == 2)
+        def _():
+            event(0, 1)
+            event(0, 2)
+
+        @pl.when(t == 6)
+        def _():
+            event(0, 3)
+
+        nb = order(t)
+
+        def against(i, carry):
+            b = order(i)
+            stats(jnp.maximum(nb, b), jnp.minimum(nb, b), False)
+            return carry
+
+        lax.fori_loop(0, t, against, 0)
+        stats(nb, nb, True)
+        return carry
+
+    lse[...] = jnp.full_like(lse, jnp.finfo(F32).min)
+    s_ref[:, :, 0:lanes] = jnp.zeros((n, blk, lanes), F32)
+    lax.fori_loop(0, n, land, 0)
+
     def forward(nb, carry):
-        mrow[...] = jnp.full_like(mrow, jnp.finfo(F32).min)
-        lrow[...] = jnp.zeros_like(lrow)
-
-        def stats(j, sc):
-            s_ref[j] = sc
-            old = mrow[...]
-            top = jnp.maximum(old, fold(sc, jnp.maximum))
-            total = lrow[...] * expo(old, top)
-            for part in groups(sc):
-                total += expo(part, top)
-            mrow[...] = top
-            lrow[...] = total
-
-        def scores(j, carry):
-            stats(j, _mm_t(q[nb], k[j]))
+        peak = lse[nb]
+        top = jnp.max(peak, axis=1, keepdims=True)
+        total = jnp.sum(s_ref[nb, :, 0:lanes] * expo(peak, top), axis=1, keepdims=True)
+        lse[nb] = jnp.broadcast_to(top + jnp.log(total) * (1.0 / scale), (blk, lanes))
+        oacc[...] = jnp.zeros_like(oacc)
+
+        def values(j, mask):
+            shift = lse[nb]
+            pr = [expo(part, shift) for part in groups(_mm_t(q[nb], k[j]))]
+            if mask:
+                pr = [jnp.where(kg, part, 0.0) for kg, part in zip(groups(keep), pr)]
+            oacc[...] += _mm(jnp.concatenate([part.astype(BF16) for part in pr], axis=1), v[j])
+
+        def below(j, carry):
+            values(j, False)
             return carry
 
-        lax.fori_loop(0, nb, scores, 0)
-        stats(nb, jnp.where(keep, _mm_t(q[nb], k[nb]), -jnp.inf))
-        top = jnp.max(mrow[...], axis=1, keepdims=True)
-        total = jnp.sum(lrow[...] * expo(mrow[...], top), axis=1, keepdims=True)
-        lse[nb] = jnp.broadcast_to(top + jnp.log(total) * (1.0 / scale), mrow.shape)
-        oacc[...] = jnp.zeros_like(oacc)
-
-        def values(j, carry):
-            shift = lse[nb]
-            pb = jnp.concatenate([expo(part, shift).astype(BF16) for part in groups(s_ref[j])], axis=1)
-            oacc[...] += _mm(pb, v[j])
-            return carry
-
-        lax.fori_loop(0, nb + 1, values, 0)
+        lax.fori_loop(0, nb, below, 0)
+        values(nb, True)
         o[nb] = oacc[...].astype(BF16)
         return carry
 
     lax.fori_loop(0, n, forward, 0)
 
     def q_step(t, carry):
-        p = t // 2
-        nb = lax.rem(me + 2 * p + 2 * (p // 2) * (1 - 2 * lax.rem(p, 2)), n) + lax.rem(t, 2) * flip
+        nb = order(t)
 
         @pl.when(t == 0)
         def _():
@@ -265,16 +294,6 @@
         @pl.when(t == 7)
         def _():
             wevent(1)
-
-        dy_copy = pltpu.make_async_copy(dyf.at[nb], xbuf.at[0], x_sem.at[0])
-
-        @pl.when(t == 0)
-        def _():
-            pltpu.make_async_copy(dy, xbuf.at[0], x_sem.at[0]).start()
-
-        @pl.when(t > 0)
-        def _():
-            dy_copy.start()
 
         qt[...] = q[nb].T
         dot_[...] = do[nb].T
@@ -313,11 +332,6 @@
         def _():
             dqr[me] = dq
 
-        dy_copy.wait()
-        ot = o[nb].T
-        for c in range(model // tile):
-            at = pl.ds(c * tile, tile)
-            dwo_v[:, at] += _mm(ot, xbuf[0, :, at])
         return carry
 
     lax.fori_loop(0, n, q_step, 0)
@@ -338,8 +352,6 @@
 
     lax.fori_loop(0, n, convert, 0)
 
-    out_wo = pltpu.make_async_copy(dwo_v, dwo, o_sem.at[0])
-    out_wo.start()
     half_chips = n // 2
 
     def stag(b):
@@ -423,6 +435,30 @@
     rs_start(acc.at[1, ob_ // 2, :, pl.ds(tile // 2, tile // 2)], dwr, 1, 1, 0)
     rs_start(acc.at[1, rb // 2, :, pl.ds(tile // 2, tile // 2)], dwr, 1, 0, 2)
     rs_start(acc.at[1, lb // 2, :, pl.ds(0, tile // 2)], dwr, 1, 1, 2)
+
+    def y_copy(b, slot):
+        return pltpu.make_async_copy(dyf.at[b], xbuf.at[slot], x_sem.at[slot])
+
+    pltpu.make_async_copy(dy, xbuf.at[0], x_sem.at[0]).start()
+
+    def y_step(i, carry):
+        slot = lax.rem(i, 2)
+        b = lax.rem(me + i, n)
+        ot = o[b].T
+        y_copy(b, slot).wait()
+
+        @pl.when(i < n - 1)
+        def _():
+            y_copy(lax.rem(me + i + 1, n), 1 - slot).start()
+
+        for c in range(model // tile):
+            at = pl.ds(c * tile, tile)
+            dwo_v[:, at] += _mm(ot, xbuf[slot, :, at])
+        return carry
+
+    lax.fori_loop(0, n, y_step, 0)
+    out_wo = pltpu.make_async_copy(dwo_v, dwo, o_sem.at[0])
+    out_wo.start()
 
     for b in range(n):
         kv_copy(b).wait_send()
@@ -596,7 +632,6 @@
                 pltpu.VMEM((2, width, tile // 2), F32),
                 pltpu.VMEM((2, rows, model), BF16),
                 pltpu.VMEM((rows, 128), F32),
-                pltpu.VMEM((rows, 128), F32),
                 pltpu.VMEM((rows, width), F32),
                 pltpu.VMEM((width, rows), BF16),
                 pltpu.VMEM((width, rows), BF16),

time: 251 us -> 248 us (0.988)
  Pallas kernels: 242 us -> 238 us
    pallas_call x1, Pallas kernels: 242 us -> 238 us  [local_grads(): pl.pallas_call(functools.partial(_kernel, n, scale), name='attention_grad...]
where the time goes in v5:
time: 248 us; the launch traced here: 247 us
  Pallas kernels  238 us (96%)
  local copies, waits for them, and re-layouts  8.39 us (3%)
    pallas_call x1, Pallas kernels, local_grads(): pl.pallas_call(functools.partial(_kernel, n, scale), name='attention_grad...  238 us
    unnamed x13, local copies, waits for them, and re-layouts  8.39 us

profile of v5, /device:TPU:113, one launch (start us, length us, event | category | flops | bytes accessed | tf_op | source)
XLA Modules:
  0.0 247.3 jit_solution(13585129847928162075)
XLA Ops:
  0.6 238.2 %attention_grads.1 = (bf16[512,2048]{1,0:T(8,128)(2,1)}, f32[8,512,128]{2,1,0:T(8,128)}, f32[256,2048]{1,0:T(8,128)}, f32[256,256]{1,0:T(8,128)}, f32[256,256]{1...) custom-call(bf16[512,2048]{1,0:T(8,128)(2,1)} %x.1, ...), custom_call_target="tpu_custom_call" | custom-call | tf_op jit(solution)/shard_map/attention_grads/pallas_call | solution.py:602
  238.9 0.0 copy-start.1
  238.9 3.3 %copy.17 = bf16[512,2048]{1,0:T(8,128)(2,1)} copy(bf16[512,2048]{1,0:T(8,128)(2,1)} %get-tuple-element.25) | data formatting | bytes 4194304
  242.2 0.0 copy-done.1
  242.2 0.0 copy-start
  242.2 1.3 copy.18
  243.5 1.0 copy-done
  244.5 0.0 copy-start.3
  244.5 0.0 copy-start.2
  244.5 1.3 copy.19
  245.8 0.0 copy-done.3
  245.9 0.7 copy.20
  246.6 0.0 copy-done.2
  246.6 0.7 copy.21
Async XLA Ops:
  238.9 3.3 %copy-start.1 = (f32[8,512,128]{2,1,0:T(8,128)S(1)}, f32[8,512,128]{2,1,0:T(8,128)}, u32[]{:S(2)}) copy-start(f32[8,512,128]{2,1,0:T(8,128)} %get-tuple-element.11) | copy-start | bytes 6291460
  242.2 2.3 copy-start
  244.5 1.3 copy-start.3
  244.5 2.0 copy-start.2

commit v6 on v5

--- a/solution.py
+++ b/solution.py
@@ -52,7 +52,7 @@
             mrow, oacc, qt, dot_, dwo_v,
             g_sr, g_sl, g_sp, g_recv, l_sem,
             w_sr, w_sl, w_sp, w_st, w_recv, dq_send, dq_recv, kv_send, kv_recv,
-            rs_send, rs_recv, x_sem, b_sem, o_sem):
+            rs_send, rs_recv, x_sem, b_sem, o_sem, y_sem):
     me, core, right, left, opp, mate = _ring(n)
     chip = me // 2
     flip = 1 - 2 * core
@@ -209,17 +209,21 @@
         p = t // 2
         return lax.rem(me + 2 * p + 2 * (p // 2) * (1 - 2 * lax.rem(p, 2)), n) + lax.rem(t, 2) * flip
 
+    def sums(nb):
+        return jnp.concatenate([dwo_v[nb, :, 0:lanes], dwo_v[nb, :, lanes:2 * lanes]], axis=0)
+
     def stats(nb, j, mask):
         sc = _mm_t(q[nb], k[j])
         if mask:
             sc = jnp.where(keep, sc, -jnp.inf)
         old = lse[nb]
         top = jnp.maximum(old, fold(sc, jnp.maximum))
-        total = s_ref[nb, :, 0:lanes] * expo(old, top)
+        total = sums(nb) * expo(old, top)
         for part in groups(sc):
             total += expo(part, top)
         lse[nb] = top
-        s_ref[nb, :, 0:lanes] = total
+        dwo_v[nb, :, 0:lanes] = total[:half]
+        dwo_v[nb, :, lanes:2 * lanes] = total[half:]
 
     def land(t, carry):
         @pl.when(t == 0)
@@ -247,29 +251,48 @@
         return carry
 
     lse[...] = jnp.full_like(lse, jnp.finfo(F32).min)
-    s_ref[:, :, 0:lanes] = jnp.zeros((n, blk, lanes), F32)
     lax.fori_loop(0, n, land, 0)
+
+    def pipelined(nb, start, work):
+        start(0, 0)
+
+        def pair(p, carry):
+            start(2 * p + 1, 1)
+            work(2 * p, 0, False)
+            start(2 * p + 2, 0)
+            work(2 * p + 1, 1, False)
+            return carry
+
+        lax.fori_loop(0, nb // 2, pair, 0)
+
+        @pl.when(lax.rem(nb, 2) == 0)
+        def _():
+            work(nb, 0, True)
+
+        @pl.when(lax.rem(nb, 2) == 1)
+        def _():
+            start(nb, 1)
+            work(nb - 1, 0, False)
+            work(nb, 1, True)
 
     def forward(nb, carry):
         peak = lse[nb]
         top = jnp.max(peak, axis=1, keepdims=True)
-        total = jnp.sum(s_ref[nb, :, 0:lanes] * expo(peak, top), axis=1, keepdims=True)
+        total = jnp.sum(sums(nb) * expo(peak, top), axis=1, keepdims=True)
         lse[nb] = jnp.broadcast_to(top + jnp.log(total) * (1.0 / scale), (blk, lanes))
         oacc[...] = jnp.zeros_like(oacc)
 
-        def values(j, mask):
+        def start(j, slot):
+            s_ref[slot] = _mm_t(q[nb], k[j])
+
+        def values(j, slot, mask):
             shift = lse[nb]
-            pr = [expo(part, shift) for part in groups(_mm_t(q[nb], k[j]))]
+            pr = [expo(part, shift) for part in groups(s_ref[slot])]
             if mask:
                 pr = [jnp.where(kg, part, 0.0) for kg, part in zip(groups(keep), pr)]
             oacc[...] += _mm(jnp.concatenate([part.astype(BF16) for part in pr], axis=1), v[j])
 
-        def below(j, carry):
-            values(j, False)
-            return carry
-
-        lax.fori_loop(0, nb, below, 0)
-        values(nb, True)
+        pipelined(nb, start, values)
         o[nb] = oacc[...].astype(BF16)
         return carry
 
@@ -290,9 +313,6 @@
         @pl.when(t == 6)
         def _():
             event(1, 3)
-
-        @pl.when(t == 7)
-        def _():
             wevent(1)
 
         qt[...] = q[nb].T
@@ -301,9 +321,13 @@
         mrow[...] = jnp.broadcast_to(delta, mrow.shape)
         oacc[...] = jnp.zeros_like(oacc)
 
-        def grads(j, mask):
-            sc = groups(_mm_t(q[nb], k[j]))
-            dp = groups(_mm_t(do[nb], v[j]))
+        def start(j, slot):
+            s_ref[slot] = _mm_t(q[nb], k[j])
+            s_ref[2 + slot] = _mm_t(do[nb], v[j])
+
+        def grads(j, slot, mask):
+            sc = groups(s_ref[slot])
+            dp = groups(s_ref[2 + slot])
             shift, less = lse[nb], mrow[...]
             pr = [expo(part, shift) for part in sc]
             if mask:
@@ -314,12 +338,7 @@
             acc[0, j] += _mm(qt[...], ds)
             acc[1, j] += _mm(dot_[...], pb)
 
-        def below(j, carry):
-            grads(j, False)
-            return carry
-
-        lax.fori_loop(0, nb, below, 0)
-        grads(nb, True)
+        pipelined(nb, start, grads)
         dq = (oacc[...] * scale).astype(BF16)
         q[nb] = dq
         lhs[nb, 0:width] = dq.T
@@ -440,6 +459,8 @@
         return pltpu.make_async_copy(dyf.at[b], xbuf.at[slot], x_sem.at[slot])
 
     pltpu.make_async_copy(dy, xbuf.at[0], x_sem.at[0]).start()
+    part_w = model // n
+    dwo_v[...] = jnp.zeros_like(dwo_v)
 
     def y_step(i, carry):
         slot = lax.rem(i, 2)
@@ -451,14 +472,15 @@
         def _():
             y_copy(lax.rem(me + i + 1, n), 1 - slot).start()
 
-        for c in range(model // tile):
-            at = pl.ds(c * tile, tile)
-            dwo_v[:, at] += _mm(ot, xbuf[slot, :, at])
+        for c in range(n):
+            dwo_v[c] += _mm(ot, xbuf[slot, :, c * part_w:(c + 1) * part_w])
         return carry
 
     lax.fori_loop(0, n, y_step, 0)
-    out_wo = pltpu.make_async_copy(dwo_v, dwo, o_sem.at[0])
-    out_wo.start()
+    outs = [pltpu.make_async_copy(dwo_v.at[c], dwo.at[:, pl.ds(c * part_w, part_w)], y_sem.at[c])
+            for c in range(n)]
+    for c in outs:
+        c.start()
 
     for b in range(n):
         kv_copy(b).wait_send()
@@ -498,13 +520,6 @@
 
         lax.fori_loop(0, n, heads, 0)
 
-    rs_wait(dwr, 1, 0, 0)
-    acc[1, rb // 2, :, part_cols(0)] += dwr[0, 0]
-    rs_start(acc.at[1, rb // 2, :, pl.ds(0, tile // 2)], dwr, 1, 0, 1)
-    rs_wait(dwr, 1, 1, 0)
-    acc[1, lb // 2, :, part_cols(1)] += dwr[1, 0]
-    rs_start(acc.at[1, lb // 2, :, pl.ds(tile // 2, tile // 2)], dwr, 1, 1, 1)
-
     def q_copy(c):
         return pltpu.make_async_copy(lse.at[pl.ds(2 * c, 2)], dwq.at[pl.ds(2 * c, 2)], l_sem.at[c])
 
@@ -523,6 +538,14 @@
     swap = _remote(stag(mate), kvx.at[0], b_sem.at[2, 0], b_sem.at[2, 1], mate)
     swap.start()
     kvx[1] = stag(me)[...]
+
+    rs_wait(dwr, 1, 0, 0)
+    acc[1, rb // 2, :, part_cols(0)] += dwr[0, 0]
+    rs_start(acc.at[1, rb // 2, :, pl.ds(0, tile // 2)], dwr, 1, 0, 1)
+    rs_wait(dwr, 1, 1, 0)
+    acc[1, lb // 2, :, part_cols(1)] += dwr[1, 0]
+    rs_start(acc.at[1, lb // 2, :, pl.ds(tile // 2, tile // 2)], dwr, 1, 1, 1)
+
     swap.wait()
     kv_first = kvx[1 - core].T
     kv_second = kvx[core].T
@@ -550,7 +573,7 @@
     out_dx = pltpu.make_async_copy(xbuf.at[0], dx, x_sem.at[0])
     out_dx.start()
 
-    outs = [out_wo, out_dx]
+    outs.append(out_dx)
     rs_wait(dwr, 1, 0, 1)
     rs_wait(dwr, 1, 1, 2)
     acc[1, base // 2, :, part_cols(0)] += dwr[0, 1] + dwr[1, 2]
@@ -635,11 +658,11 @@
                 pltpu.VMEM((rows, width), F32),
                 pltpu.VMEM((width, rows), BF16),
                 pltpu.VMEM((width, rows), BF16),
-                pltpu.VMEM((width, model), F32),
+                pltpu.VMEM((n, rows // 2, model // n), F32),
                 dma((2, 3)), dma((2, 3)), dma((2, 8)), dma((2, 2 * n)), dma((4,)),
                 dma((3,)), dma((3,)), dma((16,)), dma((6,)), dma((n, 4)),
                 dma((n,)), dma((n,)), dma((n,)), dma((n,)),
-                dma((2, 2, 3)), dma((2, 2, 3)), dma((2,)), dma((3, n)), dma((4,)),
+                dma((2, 2, 3)), dma((2, 2, 3)), dma((2,)), dma((3, n)), dma((4,)), dma((n,)),
             ],
             compiler_params=pltpu.CompilerParams(
                 collective_id=0, has_side_effects=True, vmem_limit_bytes=VMEM_MAX),

time: 248 us -> 246 us (level)
  no operation moved by 1% of the time
where the time goes in v6:
time: 246 us; the launch traced here: 245 us
  Pallas kernels  236 us (96%)
  local copies, waits for them, and re-layouts  8.39 us (3%)
    pallas_call x1, Pallas kernels, local_grads(): pl.pallas_call(functools.partial(_kernel, n, scale), name='attention_grad...  236 us
    unnamed x13, local copies, waits for them, and re-layouts  8.39 us

profile of v6, /device:TPU:113, one launch (start us, length us, event | category | flops | bytes accessed | tf_op | source)
XLA Modules:
  0.0 245.2 jit_solution(10778749693265963682)
XLA Ops:
  0.6 236.2 %attention_grads.1 = (bf16[512,2048]{1,0:T(8,128)(2,1)}, f32[8,512,128]{2,1,0:T(8,128)}, f32[256,2048]{1,0:T(8,128)}, f32[256,256]{1,0:T(8,128)}, f32[256,256]{1...) custom-call(bf16[512,2048]{1,0:T(8,128)(2,1)} %x.1, ...), custom_call_target="tpu_custom_call" | custom-call | tf_op jit(solution)/shard_map/attention_grads/pallas_call | solution.py:625
  236.8 0.0 copy-start.1
  236.9 3.3 %copy.17 = bf16[512,2048]{1,0:T(8,128)(2,1)} copy(bf16[512,2048]{1,0:T(8,128)(2,1)} %get-tuple-element.25) | data formatting | bytes 4194304
  240.2 0.0 copy-done.1
  240.2 0.0 copy-start
  240.2 1.3 copy.18
  241.5 1.0 copy-done
  242.5 0.0 copy-start.3
  242.5 0.0 copy-start.2
  242.5 1.3 copy.19
  243.8 0.0 copy-done.3
  243.8 0.7 copy.20
  244.5 0.0 copy-done.2
  244.5 0.7 copy.21
Async XLA Ops:
  236.8 3.3 %copy-start.1 = (f32[8,512,128]{2,1,0:T(8,128)S(1)}, f32[8,512,128]{2,1,0:T(8,128)}, u32[]{:S(2)}) copy-start(f32[8,512,128]{2,1,0:T(8,128)} %get-tuple-element.11) | copy-start | bytes 6291460
  240.2 2.3 copy-start
  242.5 1.3 copy-start.3
  242.5 2.0 copy-start.2

commit v7 on v6

--- a/solution.py
+++ b/solution.py
@@ -156,8 +156,9 @@
 
     def send_wq():
         for i in range(2):
-            wcopy(wown(mine + i), me, mine + i, w_sr.at[i], right).start()
-            wcopy(wown(mine + 1 - i), me, mine + 1 - i, w_sl.at[i], left).start()
+            for g, sems, dev in ((i, w_sr, right), (1 - i, w_sl, left)):
+                src = wq_v.at[pl.ds((mine + g) * quarter, quarter)]
+                wcopy(src, me, mine + g, sems.at[i], dev).start()
 
     def wevent(e):
         pieces = (((left, 0), (right, 1)), ((left, 1), (right, 0)), ((opp, 0), (opp, 1)))[e - 1]

time: 246 us -> 246 us (level)
  no operation moved by 1% of the time
where the time goes in v7:
time: 246 us; the launch traced here: 245 us
  Pallas kernels  236 us (96%)
  local copies, waits for them, and re-layouts  8.39 us (3%)
    pallas_call x1, Pallas kernels, local_grads(): pl.pallas_call(functools.partial(_kernel, n, scale), name='attention_grad...  236 us
    unnamed x13, local copies, waits for them, and re-layouts  8.39 us

profile of v7, /device:TPU:113, one launch (start us, length us, event | category | flops | bytes accessed | tf_op | source)
XLA Modules:
  0.0 245.2 jit_solution(1742788850461162944)
XLA Ops:
  0.6 236.2 %attention_grads.1 = (bf16[512,2048]{1,0:T(8,128)(2,1)}, f32[8,512,128]{2,1,0:T(8,128)}, f32[256,2048]{1,0:T(8,128)}, f32[256,256]{1,0:T(8,128)}, f32[256,256]{1...) custom-call(bf16[512,2048]{1,0:T(8,128)(2,1)} %x.1, ...), custom_call_target="tpu_custom_call" | custom-call | tf_op jit(solution)/shard_map/attention_grads/pallas_call | solution.py:626
  236.8 0.0 copy-start.1
  236.9 3.3 %copy.17 = bf16[512,2048]{1,0:T(8,128)(2,1)} copy(bf16[512,2048]{1,0:T(8,128)(2,1)} %get-tuple-element.25) | data formatting | bytes 4194304
  240.2 0.0 copy-done.1
  240.2 0.0 copy-start
  240.2 1.3 copy.18
  241.5 1.0 copy-done
  242.5 0.0 copy-start.3
  242.5 0.0 copy-start.2
  242.5 1.3 copy.19
  243.8 0.0 copy-done.3
  243.8 0.7 copy.20
  244.5 0.0 copy-done.2
  244.5 0.7 copy.21
Async XLA Ops:
  236.8 3.3 %copy-start.1 = (f32[8,512,128]{2,1,0:T(8,128)S(1)}, f32[8,512,128]{2,1,0:T(8,128)}, u32[]{:S(2)}) copy-start(f32[8,512,128]{2,1,0:T(8,128)} %get-tuple-element.11) | copy-start | bytes 6291460
  240.2 2.3 copy-start
  242.5 1.3 copy-start.3
  242.5 2.0 copy-start.2
